TPU v7x, 128 devices: a whole 4x4x4 slice. The times are simulated.
128 devices in a mesh: dp: 4 (over y_hi, core), seq: 32 (over y_lo, x, z).
Axes of the slice: x: 4, y: 4 (y_hi: 2, y_lo: 2; y = y_hi * 2 + y_lo), z: 4, core: 2. Of those that a mesh axis runs over, the one named last changes fastest.
Arguments:
- queries: bfloat16 [131072, 1024], P(('dp', 'seq')), parts along dimension 0, may hold values from -6 to 6
- keys: bfloat16 [131072, 1024], P(('dp', 'seq')), parts along dimension 0, may hold values from -6 to 6
- values: bfloat16 [131072, 1024], P(('dp', 'seq')), parts along dimension 0, may hold values from -6 to 6
Outputs:
- attended: bfloat16 [131072, 1024], P(('dp', 'seq')), parts along dimension 0
- far_attended: bfloat16 [4096, 1024], P(('dp', 'seq')), parts along dimension 0
There are 4 independent parts, one for each index of `dp`. A program takes and returns all parts, laid end to end along the dimension named above; each array names one. Nothing has to cross between parts.
All inputs are finite; a program needn't handle non-finite values.
Results may differ from a plain program's by a relative error of at most 0.0095.
Values may be sent and summed in bfloat16 or wider, within the bound.
No kernel may reach another device: no remote copies, remote signals or barrier semaphores. Data moves between devices by JAX's collectives and lax.ppermute only.
A program may use at most 192 MiB of HBM per device.

v0:
```python
import jax
import jax.numpy as jnp
import numpy as np
from jax import lax
from jax.sharding import PartitionSpec as P

H = 16
HD = 64
MIDDLE_DILATION = 4
OUTER_DILATION = 32


VOID_LEVEL = -1e30


def joined_along(pieces, dim):
    pieces = jnp.moveaxis(pieces, 0, dim)
    lengths = pieces.shape
    return pieces.reshape(*lengths[:dim], lengths[dim] * lengths[dim + 1], *lengths[dim + 2 :])


def one_gather(arrays, axis, dims):
    vector = jnp.concatenate([a.reshape(-1) for a in arrays])
    lines, at, finished = (lax.all_gather(vector, axis), 0, [])
    for a, dim in zip(arrays, dims):
        pieces = lines[:, at : at + a.size].reshape(-1, *a.shape)
        finished.append(joined_along(pieces, dim))
        at += a.size
    return tuple(finished)


def as_sent(array):

    def short(part):
        return part.astype(jnp.bfloat16) if part.dtype == jnp.float32 else part

    return jax.tree.map(short, array)


def partner(block, axis, stride):
    count = lax.axis_size(axis)
    route = []
    for low in range(count):
        high = low | 1 << stride
        if high != low and high < count:
            route += [(low, high), (high, low)]
    return lax.ppermute(block, axis, route)


def attend_one(query, keys, values):
    factor = query.shape[-1] ** (-0.5)
    scores = jnp.einsum("qd,kd->qk", query, keys, preferred_element_type=jnp.float32) * factor
    peak = jnp.max(scores, axis=-1, keepdims=True)
    powers = jnp.exp(scores - peak)
    total = jnp.sum(powers, axis=-1, keepdims=True)
    mixed = (
        jnp.einsum(
            "qk,kd->qd", powers.astype(jnp.bfloat16), values, preferred_element_type=jnp.float32
        )
        / total
    )
    return (mixed.astype(jnp.bfloat16), peak[:, 0] + jnp.log(total[:, 0]))


def attend_per_head(query, keys, values):
    return lax.map(
        lambda triple: attend_one(triple[0], triple[1], triple[2]), (query, keys, values)
    )


def to_heads(array):
    length = array.shape[0]
    return array.reshape(length, H, HD).transpose(1, 0, 2)


def dilate_tokens(array, rate):
    heads, length, depth = array.shape
    offsets = np.arange(heads) % rate
    return array.reshape(heads, length // rate, rate, depth)[np.arange(heads), :, offsets, :]


def spread_back(mixed, level, rate):
    heads, count, depth = mixed.shape
    chosen = np.arange(rate)[None, :] == (np.arange(heads) % rate)[:, None]
    full_out = (
        mixed.astype(jnp.float32)[:, :, None, :] * chosen.astype(np.float32)[:, None, :, None]
    ).reshape(heads, count * rate, depth)
    full_level = jnp.where(chosen[:, None, :], level[:, :, None], VOID_LEVEL).reshape(
        heads, count * rate
    )
    return (full_out, full_level)


def combine_levels(branches):
    peak = branches[0][1]
    for entry in branches[1:]:
        peak = jnp.maximum(peak, entry[1])
    numer = jnp.zeros(branches[0][0].shape, jnp.float32)
    denom = jnp.zeros(peak.shape, jnp.float32)
    for entry in branches:
        weight = jnp.exp(entry[1] - peak)
        numer = numer + weight[..., None] * entry[0].astype(jnp.float32)
        denom = denom + weight
    return numer / denom[..., None]


def far_gather(distant_key, distant_value):
    return one_gather((distant_key, distant_value), "seq", (1, 1))


def level_parts(level):
    upper_part = level.astype(jnp.bfloat16)
    rest = level - upper_part.astype(jnp.float32)
    middle_part = rest.astype(jnp.bfloat16)
    lower_part = (rest - middle_part.astype(jnp.float32)).astype(jnp.bfloat16)
    return (upper_part, middle_part, lower_part)


def owner_heads(central_query, central_key, central_value, member, bits):
    count = central_query.shape[1]
    leading = (2,) * bits
    arrays = tuple(
        (
            array.reshape(leading + (H >> bits, count, HD))
            for array in (central_query, central_key, central_value)
        )
    )
    for bit_pos in range(bits):
        is_upper = member >> bit_pos & 1 == 1
        bit_axis = bits - 1 - bit_pos
        lowers = tuple((jnp.take(array, 0, axis=bit_axis) for array in arrays))
        uppers = tuple((jnp.take(array, 1, axis=bit_axis) for array in arrays))
        kept_part = tuple(
            (
                jnp.where(is_upper, upper_part, lower_part)
                for lower_part, upper_part in zip(lowers, uppers)
            )
        )
        sent_part = tuple(
            (
                jnp.where(is_upper, lower_part, upper_part)
                for lower_part, upper_part in zip(lowers, uppers)
            )
        )
        arrived = jax.tree.map(
            lambda part, own: part.astype(own.dtype),
            partner(as_sent(sent_part), "seq", bit_pos),
            sent_part,
        )
        arrays = tuple(
            (
                jnp.where(
                    is_upper,
                    jnp.concatenate([got_part, own_part], axis=-2),
                    jnp.concatenate([own_part, got_part], axis=-2),
                )
                for own_part, got_part in zip(kept_part, arrived)
            )
        )
    mixed, level = attend_per_head(arrays[0], arrays[1], arrays[2])
    pieces = (mixed,) + level_parts(level)
    for bit_pos in reversed(range(bits)):
        is_upper = member >> bit_pos & 1 == 1
        half_rows = pieces[1].shape[-1] // 2
        lowers = (pieces[0][..., :half_rows, :],) + tuple(
            (piece[..., :half_rows] for piece in pieces[1:])
        )
        uppers = (pieces[0][..., half_rows:, :],) + tuple(
            (piece[..., half_rows:] for piece in pieces[1:])
        )
        kept_part = tuple(
            (
                jnp.where(is_upper, upper_part, lower_part)
                for lower_part, upper_part in zip(lowers, uppers)
            )
        )
        sent_part = tuple(
            (
                jnp.where(is_upper, lower_part, upper_part)
                for lower_part, upper_part in zip(lowers, uppers)
            )
        )
        got_out, got_upper, got_middle, got_lower = partner(
            (sent_part[0], sent_part[1], sent_part[2], sent_part[3]), "seq", bit_pos
        )
        arrived = (got_out, got_upper, got_middle, got_lower)
        pieces = tuple(
            (
                jnp.where(
                    is_upper, jnp.stack([got_part, own_part]), jnp.stack([own_part, got_part])
                )
                for own_part, got_part in zip(kept_part, arrived)
            )
        )
    order = tuple(reversed(range(bits)))
    mixed = pieces[0].transpose(order + (bits, bits + 1, bits + 2)).reshape(H, count, HD)
    level = jnp.zeros((H, count), jnp.float32)
    for piece in pieces[1:]:
        level = level + piece.transpose(order + (bits, bits + 1)).reshape(H, count).astype(
            jnp.float32
        )
    return (mixed, level)


def per_device(queries, keys, values):
    row_count = queries.shape[0]
    query_per_head = to_heads(queries)
    key_per_head = to_heads(keys)
    value_per_head = to_heads(values)
    pair_key, pair_value = partner((key_per_head, value_per_head), "seq", 0)
    local_output, local_level = attend_per_head(
        query_per_head,
        jnp.concatenate([key_per_head, pair_key], axis=1),
        jnp.concatenate([value_per_head, pair_value], axis=1),
    )
    central_query = dilate_tokens(query_per_head, MIDDLE_DILATION)
    central_key = dilate_tokens(key_per_head, MIDDLE_DILATION)
    central_value = dilate_tokens(value_per_head, MIDDLE_DILATION)
    distant_query = dilate_tokens(query_per_head, OUTER_DILATION)
    distant_key = dilate_tokens(key_per_head, OUTER_DILATION)
    distant_value = dilate_tokens(value_per_head, OUTER_DILATION)
    total_bits = lax.axis_size("seq").bit_length() - 1
    group_bits = min(4, total_bits)
    member = lax.axis_index("seq") % (1 << group_bits)
    central_output, central_level = owner_heads(
        central_query, central_key, central_value, member, group_bits
    )
    all_key, all_value = far_gather(distant_key, distant_value)
    distant_output, distant_level = attend_per_head(distant_query, all_key, all_value)
    merged_output = combine_levels(
        [
            (local_output, local_level),
            spread_back(central_output, central_level, MIDDLE_DILATION),
            spread_back(distant_output, distant_level, OUTER_DILATION),
        ]
    )
    far_rows = distant_output.transpose(1, 0, 2).reshape(row_count // OUTER_DILATION, H * HD)
    return (
        merged_output.transpose(1, 0, 2).reshape(row_count, H * HD).astype(jnp.bfloat16),
        far_rows,
    )


def solution(mesh):
    return jax.shard_map(
        per_device,
        mesh=mesh,
        in_specs=(P(("dp", "seq"), None), P(("dp", "seq"), None), P(("dp", "seq"), None)),
        out_specs=(P(("dp", "seq"), None), P(("dp", "seq"), None)),
        check_vma=False,
    )
```

profile of v0, /device:TPU:56, one launch (start us, length us, event | category | flops | bytes accessed | tf_op | source)
XLA Modules:
  0.0 616.4 jit_solution(4940527589438615590)
XLA Ops:
  15.2 5.9 copy.394
  29.3 6.2 %copy.346 = bf16[16,1024,64]{2,0,1:T(8,128)(2,1)} copy(bf16[16,1024,64]{1,2,0:T(8,128)(2,1)} %bitcast.389) | data formatting | bytes 4194304 | tf_op jit(solution)/shard_map/transpose | solution.py:73
  35.4 6.0 copy.347
  50.4 6.2 %copy.354 = bf16[16,1024,64]{2,0,1:T(8,128)(2,1)} copy(bf16[16,1024,64]{1,2,0:T(8,128)(2,1)} %bitcast.384) | data formatting | bytes 4194304 | tf_op jit(solution)/shard_map/transpose | solution.py:73
  56.6 6.0 copy.355
  73.9 6.0 copy.384
  82.8 6.0 copy.386
  97.3 6.0 copy.382
  112.9 14.8 %collective-permute-done.6 = bf16[2,2,2,1,256,64]{4,5,0,1,3,2:T(8,128)(2,1)} collective-permute-done((bf16[2,2,2,1,256,64]{4,5,0,1,3,2:T(8,128)(2,1)}, bf16[2,2,2,1,256,64]{4,5,0,1,3,2:T(8,128)(2,1)}, u32[]{:S(2)}, u32[]{:S(2)}) %collective-permute-start.6) | collective-permute-done | bytes 262176 | tf_op jit(solution)/shard_map/ppermute | solution.py:47
  157.3 6.6 %collective-permute-done.8 = bf16[2,1,1024,64]{2,3,1,0:T(8,128)(2,1)S(1)} collective-permute-done((bf16[2,1,1024,64]{2,3,1,0:T(8,128)(2,1)S(1)}, bf16[2,1,1024,64]{2,3,1,0:T(8,128)(2,1)S(1)}, u32[]{:S(2)}, u32[]{:S(2)}) %collective-permute-start.8) | collective-permute-done | bytes 262176 | tf_op jit(solution)/shard_map/ppermute | solution.py:47
  175.1 23.3 %multiply_reduce_fusion.1 = (f32[4096]{0:T(1024)S(1)}, f32[4096,4096]{0,1:T(8,128)}) fusion(bf16[2048,64]{0,1:T(8,128)(2,1)S(1)} %get-tuple-element.270, bf16[2048,64]{0,1:T(8,128)(2,1)S(1)} %bitcast.419, pred[]{:T(512)S(6)} %eq.21, bf16[2048,64]{0,1:T(8,128)(2,1)S(1)} %get-tuple-element.255, bf16[2048,64]{0,1:T(8,128)(2,1)S(1)} %bitcast.418), kind=kOutput, calls=%fused_computation.45 | convolution fusion | flops 2185752576 | bytes 68173824 | tf_op jit(solution)/shard_map/while/body/eval_jaxpr/qd,kd->qk/dot_general | solution.py:52
  198.5 21.6 %fusion.42 = f32[4096]{0:T(1024)S(1)} fusion(f32[4096,4096]{0,1:T(8,128)} %get-tuple-element.310, f32[4096]{0:T(1024)S(1)} %get-tuple-element.309), kind=kLoop, calls=%fused_computation.47 | loop fusion | flops 50327552 | bytes 67141632 | tf_op jit(solution)/shard_map/while/body/eval_jaxpr/reduce_sum | solution.py:55
  220.1 23.7 %fusion.57 = bf16[1,4096,64]{1,2,0:T(8,128)(2,1)S(1)} fusion(f32[4096,4096]{0,1:T(8,128)} %get-tuple-element.310, f32[4096]{0:T(1024)S(1)} %get-tuple-element.309, bf16[2048,64]{0,1:T(8,128)(2,1)S(1)} %get-tuple-element.253, bf16[2048,64]{0,1:T(8,128)(2,1)S(1)} %bitcast.420, f32[4096]{0:T(1024)S(1)} %fusion.42, pred[]{:T(512)S(6)} %eq.21), kind=kOutput, calls=%fused_computation.59 | convolution fusion | flops 2200698880 | bytes 68190208 | tf_op jit(solution)/shard_map/while/body/eval_jaxpr/qk,kd->qd/dot_general | solution.py:57
  261.5 10.1 %collective-permute-start.20 = (bf16[2,2,1,512]{3,1,2,0:T(2,128)(2,1)S(1)}, bf16[2,2,1,512]{3,1,2,0:T(2,128)(2,1)S(1)}, u32[]{:S(2)}, u32[]{:S(2)}) collective-permute-start(bf16[2,2,1,512]{3,1,2,0:T(2,128)(2,1)S(1)} %get-tuple-element.295), channel_id=1, source_target_pairs={{0,2},{2,0},{1,3},{3,1},{4,6},{6,4},{5,7},{7,5},{8,10},{10,8},{9,1... | collective-permute-start | bytes 12296 | tf_op jit(solution)/shard_map/ppermute | solution.py:47
  286.1 6.3 %collective-permute-done.27 = bf16[2,1,1024,64]{2,3,0,1:T(8,128)(2,1)S(1)} collective-permute-done((bf16[2,1,1024,64]{2,3,0,1:T(8,128)(2,1)S(1)}, bf16[2,1,1024,64]{2,3,0,1:T(8,128)(2,1)S(1)}, u32[]{:S(2)}, u32[]{:S(2)}) %collective-permute-start.27) | collective-permute-done | bytes 262176 | tf_op jit(solution)/shard_map/ppermute | solution.py:47
  312.3 183.1 %while.37 = (s32[]{:T(128)}, bf16[16,1024,64]{1,2,0:T(8,128)(2,1)}, f32[16,1024]{1,0:T(8,128)S(1)}, bf16[16,1024,64]{2,1,0:T(8,128)(2,1)}, bf16[16,2048,64]{1,2,...) while((s32[]{:T(128)}, bf16[16,1024,64]{1,2,0:T(8,128)(2,1)}, ...), condition=%wide.region_3.4_spmd, body=%wide.region_0.3_spmd.sunk | while | flops 553778176 | bytes 59680884 | solution.py:66
  329.4 5.7 fusion.126
  340.9 5.7 fusion.126
  352.3 5.7 fusion.126
  363.8 5.7 fusion.126
  375.2 5.7 fusion.126
  398.1 5.7 fusion.126
  409.5 5.7 fusion.126
  421.0 5.7 fusion.126
  432.5 5.7 fusion.126
  444.0 5.7 fusion.126
  466.8 5.7 fusion.126
  478.3 5.7 fusion.126
  498.1 6.2 %copy.390 = bf16[16,1024,64]{2,0,1:T(8,128)(2,1)} copy(bf16[16,1024,64]{1,2,0:T(8,128)(2,1)} %get-tuple-element.96) | data formatting | bytes 4194304 | tf_op jit(solution)/shard_map/while | solution.py:66
  513.7 6.5 %reshape.1863 = bf16[32,16,32,64]{3,2,1,0:T(8,128)(2,1)} reshape(bf16[32,32768]{1,0:T(8,128)(2,1)} %get-tuple-element.251) | data formatting | bytes 4194304 | tf_op jit(solution)/shard_map/reshape | solution.py:26
  536.5 43.9 %while.38 = (s32[]{:T(128)}, bf16[16,32,64]{2,1,0:T(8,128)(2,1)S(1)}, f32[16,32]{1,0:T(8,128)S(1)}, bf16[16,32,64]{2,1,0:T(8,128)(2,1)}, bf16[16,1024,64]{2,1,0:...) while((s32[]{:T(128)}, bf16[16,32,64]{2,1,0:T(8,128)(2,1)S(1)}, ...), condition=%wide.region_9.18_spmd, body=%wide.region_6.17_spmd.sunk | while | flops 8589282 | bytes 938073 | solution.py:66
  586.3 15.3 %fusion.50 = bf16[16,1024,64]{2,0,1:T(8,128)(2,1)} fusion(f32[16,1024,64]{2,1,0:T(8,128)S(1)} %bitcast.387, bf16[16,1024,64]{2,0,1:T(8,128)(2,1)S(1)} %copy-done.2, f32[16,1024]{0,1:T(8,128)S(1)} %copy-done.5, f32[16,1024]{0,1:T(8,128)S(1)} %bitcast.409, f32[16,1024]{0,1:T(8,128)S(1)} %copy-done.4, f32[16,1024]{0,1:T(8,128)S(1)} %bitcast.408, ...), kind=kLoop, calls=%fused_computation.56 | loop fusion | flops 10485760 | bytes 9830400 | tf_op jit(solution)/shard_map/convert_element_type | solution.py:239
  (375 shorter events, 349.6 us)
Async XLA Ops:
  7.2 497.1 %all-gather.3.cloned.1.call-start = ((), (), s32[]{:S(2)}) async-start(), calls=%async_computation | async-start | bytes 4325376 | tf_op jit(solution)/shard_map/all_gather | solution.py:24
  10.1 298.1 %collective-permute-start.1 = (bf16[16,1024,64]{1,2,0:T(8,128)(2,1)S(1)}, bf16[16,1024,64]{1,2,0:T(8,128)(2,1)}, u32[]{:S(2)}, u32[]{:S(2)}) collective-permute-start(bf16[16,1024,64]{1,2,0:T(8,128)(2,1)S(1)} %bitcast.379), channel_id=1, source_target_pairs={{0,1},{1,0},{2,3},{3,2},{4,5},{5,4},{6,7},{7,6},{8,9},{9,8},{10,11... | collective-permute-start | bytes 6291464 | tf_op jit(solution)/shard_map/ppermute | solution.py:47
  23.3 83.4 %collective-permute-start.22 = (bf16[2,2,2,1,256,64]{4,5,2,1,0,3:T(8,128)(2,1)S(1)}, bf16[2,2,2,1,256,64]{4,5,2,1,0,3:T(8,128)(2,1)}, u32[]{:S(2)}, u32[]{:S(2)}) collective-permute-start(bf16[2,2,2,1,256,64]{4,5,2,1,0,3:T(8,128)(2,1)S(1)} %get-tuple-element.267), channel_id=1, source_target_pairs={{0,1},{1,0},{2,3},{3,2},{4,5},{5,4},{6,7},{7,6},{8,9},{9,8},{10,11... | collective-permute-start | bytes 786440 | tf_op jit(solution)/shard_map/ppermute | solution.py:47
  44.4 66.9 %collective-permute-start.2 = (bf16[2,2,2,1,256,64]{4,5,0,1,3,2:T(8,128)(2,1)}, bf16[2,2,2,1,256,64]{4,5,0,1,3,2:T(8,128)(2,1)}, u32[]{:S(2)}, u32[]{:S(2)}) collective-permute-start(bf16[2,2,2,1,256,64]{4,5,0,1,3,2:T(8,128)(2,1)} %get-tuple-element.281), channel_id=1, source_target_pairs={{0,1},{1,0},{2,3},{3,2},{4,5},{5,4},{6,7},{7,6},{8,9},{9,8},{10,11... | collective-permute-start | bytes 786440 | tf_op jit(solution)/shard_map/ppermute | solution.py:47
  48.4 255.5 %collective-permute-start = (bf16[16,1024,64]{1,2,0:T(8,128)(2,1)}, bf16[16,1024,64]{1,2,0:T(8,128)(2,1)}, u32[]{:S(2)}, u32[]{:S(2)}) collective-permute-start(bf16[16,1024,64]{1,2,0:T(8,128)(2,1)} %bitcast.383), channel_id=1, source_target_pairs={{0,1},{1,0},{2,3},{3,2},{4,5},{5,4},{6,7},{7,6},{8,9},{9,8},{10,11... | collective-permute-start | bytes 6291464 | tf_op jit(solution)/shard_map/ppermute | solution.py:47
  65.5 62.2 %collective-permute-start.6 = (bf16[2,2,2,1,256,64]{4,5,0,1,3,2:T(8,128)(2,1)}, bf16[2,2,2,1,256,64]{4,5,0,1,3,2:T(8,128)(2,1)}, u32[]{:S(2)}, u32[]{:S(2)}) collective-permute-start(bf16[2,2,2,1,256,64]{4,5,0,1,3,2:T(8,128)(2,1)} %get-tuple-element.275), channel_id=1, source_target_pairs={{0,1},{1,0},{2,3},{3,2},{4,5},{5,4},{6,7},{7,6},{8,9},{9,8},{10,11... | collective-permute-start | bytes 786440 | tf_op jit(solution)/shard_map/ppermute | solution.py:47
  108.0 30.9 %collective-permute-start.23 = (bf16[2,2,1,512,64]{3,4,0,1,2:T(8,128)(2,1)S(1)}, bf16[2,2,1,512,64]{3,4,0,1,2:T(8,128)(2,1)S(1)}, u32[]{:S(2)}, u32[]{:S(2)}) collective-permute-start(bf16[2,2,1,512,64]{3,4,0,1,2:T(8,128)(2,1)S(1)} %copy_select_fusion.2), channel_id=1, source_target_pairs={{0,2},{2,0},{1,3},{3,1},{4,6},{6,4},{5,7},{7,5},{8,10},{10,8},{9,1... | collective-permute-start | bytes 786440 | tf_op jit(solution)/shard_map/ppermute | solution.py:47
  112.5 34.2 %collective-permute-start.3 = (bf16[2,2,1,512,64]{3,4,0,1,2:T(8,128)(2,1)S(1)}, bf16[2,2,1,512,64]{3,4,0,1,2:T(8,128)(2,1)S(1)}, u32[]{:S(2)}, u32[]{:S(2)}) collective-permute-start(bf16[2,2,1,512,64]{3,4,0,1,2:T(8,128)(2,1)S(1)} %get-tuple-element.279), channel_id=1, source_target_pairs={{0,2},{2,0},{1,3},{3,1},{4,6},{6,4},{5,7},{7,5},{8,10},{10,8},{9,1... | collective-permute-start | bytes 786440 | tf_op jit(solution)/shard_map/ppermute | solution.py:47
  128.9 24.1 %collective-permute-start.7 = (bf16[2,2,1,512,64]{3,4,0,2,1:T(8,128)(2,1)S(1)}, bf16[2,2,1,512,64]{3,4,0,2,1:T(8,128)(2,1)S(1)}, u32[]{:S(2)}, u32[]{:S(2)}) collective-permute-start(bf16[2,2,1,512,64]{3,4,0,2,1:T(8,128)(2,1)S(1)} %get-tuple-element.273), channel_id=1, source_target_pairs={{0,2},{2,0},{1,3},{3,1},{4,6},{6,4},{5,7},{7,5},{8,10},{10,8},{9,1... | collective-permute-start | bytes 786440 | tf_op jit(solution)/shard_map/ppermute | solution.py:47
  139.0 27.4 %collective-permute-start.24 = (bf16[2,1,1024,64]{2,3,0,1:T(8,128)(2,1)S(1)}, bf16[2,1,1024,64]{2,3,0,1:T(8,128)(2,1)S(1)}, u32[]{:S(2)}, u32[]{:S(2)}) collective-permute-start(bf16[2,1,1024,64]{2,3,0,1:T(8,128)(2,1)S(1)} %get-tuple-element.263), channel_id=1, source_target_pairs={{0,4},{4,0},{1,5},{5,1},{2,6},{6,2},{3,7},{7,3},{8,12},{12,8},{9,1... | collective-permute-start | bytes 786440 | tf_op jit(solution)/shard_map/ppermute | solution.py:47
  146.9 9.8 %collective-permute-start.4 = (bf16[2,1,1024,64]{2,3,0,1:T(8,128)(2,1)S(1)}, bf16[2,1,1024,64]{2,3,0,1:T(8,128)(2,1)S(1)}, u32[]{:S(2)}, u32[]{:S(2)}) collective-permute-start(bf16[2,1,1024,64]{2,3,0,1:T(8,128)(2,1)S(1)} %get-tuple-element.256), channel_id=1, source_target_pairs={{0,4},{4,0},{1,5},{5,1},{2,6},{6,2},{3,7},{7,3},{8,12},{12,8},{9,1... | collective-permute-start | bytes 786440 | tf_op jit(solution)/shard_map/ppermute | solution.py:47
  153.2 10.7 %collective-permute-start.8 = (bf16[2,1,1024,64]{2,3,1,0:T(8,128)(2,1)S(1)}, bf16[2,1,1024,64]{2,3,1,0:T(8,128)(2,1)S(1)}, u32[]{:S(2)}, u32[]{:S(2)}) collective-permute-start(bf16[2,1,1024,64]{2,3,1,0:T(8,128)(2,1)S(1)} %get-tuple-element.271), channel_id=1, source_target_pairs={{0,4},{4,0},{1,5},{5,1},{2,6},{6,2},{3,7},{7,3},{8,12},{12,8},{9,1... | collective-permute-start | bytes 786440 | tf_op jit(solution)/shard_map/ppermute | solution.py:47
  156.9 12.6 %collective-permute-start.5 = (bf16[1,2048,64]{1,2,0:T(8,128)(2,1)S(1)}, bf16[1,2048,64]{1,2,0:T(8,128)(2,1)S(1)}, u32[]{:S(2)}, u32[]{:S(2)}) collective-permute-start(bf16[1,2048,64]{1,2,0:T(8,128)(2,1)S(1)} %get-tuple-element.254), channel_id=1, source_target_pairs={{0,8},{8,0},{1,9},{9,1},{2,10},{10,2},{3,11},{11,3},{4,12},{12,4},... | collective-permute-start | bytes 786440 | tf_op jit(solution)/shard_map/ppermute | solution.py:47
  164.1 11.0 %collective-permute-start.9 = (bf16[1,2048,64]{1,2,0:T(8,128)(2,1)S(1)}, bf16[1,2048,64]{1,2,0:T(8,128)(2,1)S(1)}, u32[]{:S(2)}, u32[]{:S(2)}) collective-permute-start(bf16[1,2048,64]{1,2,0:T(8,128)(2,1)S(1)} %get-tuple-element.269), channel_id=1, source_target_pairs={{0,8},{8,0},{1,9},{9,1},{2,10},{10,2},{3,11},{11,3},{4,12},{12,4},... | collective-permute-start | bytes 786440 | tf_op jit(solution)/shard_map/ppermute | solution.py:47
  166.6 53.5 %collective-permute-start.25 = (bf16[1,2048,64]{1,2,0:T(8,128)(2,1)S(1)}, bf16[1,2048,64]{1,2,0:T(8,128)(2,1)S(1)}, u32[]{:S(2)}, u32[]{:S(2)}) collective-permute-start(bf16[1,2048,64]{1,2,0:T(8,128)(2,1)S(1)} %get-tuple-element.252), channel_id=1, source_target_pairs={{0,8},{8,0},{1,9},{9,1},{2,10},{10,2},{3,11},{11,3},{4,12},{12,4},... | collective-permute-start | bytes 786440 | tf_op jit(solution)/shard_map/ppermute | solution.py:47
  243.8 52.4 %copy-start.11 = (pred[16,4]{0,1:T(4,128)(4,1)S(1)}, pred[16,4]{0,1:T(4,128)(4,1)}, u32[]{:S(2)}) copy-start(pred[16,4]{0,1:T(4,128)(4,1)} %constant.402) | copy-start | bytes 196
  243.9 41.9 %collective-permute-start.26 = (bf16[1,2048,64]{1,2,0:T(8,128)(2,1)S(1)}, bf16[1,2048,64]{1,2,0:T(8,128)(2,1)S(1)}, u32[]{:S(2)}, u32[]{:S(2)}) collective-permute-start(bf16[1,2048,64]{1,2,0:T(8,128)(2,1)S(1)} %get-tuple-element.261), channel_id=1, source_target_pairs={{0,8},{8,0},{1,9},{9,1},{2,10},{10,2},{3,11},{11,3},{4,12},{12,4},... | collective-permute-start | bytes 786440 | tf_op jit(solution)/shard_map/ppermute | solution.py:47
  247.5 5.2 collective-permute-start.18
  247.6 8.1 %collective-permute-start.14 = (bf16[1,2048]{1,0:T(2,128)(2,1)S(1)}, bf16[1,2048]{1,0:T(2,128)(2,1)S(1)}, u32[]{:S(2)}, u32[]{:S(2)}) collective-permute-start(bf16[1,2048]{1,0:T(2,128)(2,1)S(1)} %get-tuple-element.289), channel_id=1, source_target_pairs={{0,8},{8,0},{1,9},{9,1},{2,10},{10,2},{3,11},{11,3},{4,12},{12,4},... | collective-permute-start | bytes 12296 | tf_op jit(solution)/shard_map/ppermute | solution.py:47
  252.7 5.2 collective-permute-start.10
  255.7 3.7 collective-permute-start.19
  257.9 3.6 collective-permute-start.15
  259.4 12.3 %collective-permute-start.11 = (bf16[2,1,1024]{2,0,1:T(2,128)(2,1)S(1)}, bf16[2,1,1024]{2,0,1:T(2,128)(2,1)S(1)}, u32[]{:S(2)}, u32[]{:S(2)}) collective-permute-start(bf16[2,1,1024]{2,0,1:T(2,128)(2,1)S(1)} %get-tuple-element.307), channel_id=1, source_target_pairs={{0,4},{4,0},{1,5},{5,1},{2,6},{6,2},{3,7},{7,3},{8,12},{12,8},{9,1... | collective-permute-start | bytes 12296 | tf_op jit(solution)/shard_map/ppermute | solution.py:47
  261.5 15.7 %collective-permute-start.20 = (bf16[2,2,1,512]{3,1,2,0:T(2,128)(2,1)S(1)}, bf16[2,2,1,512]{3,1,2,0:T(2,128)(2,1)S(1)}, u32[]{:S(2)}, u32[]{:S(2)}) collective-permute-start(bf16[2,2,1,512]{3,1,2,0:T(2,128)(2,1)S(1)} %get-tuple-element.295), channel_id=1, source_target_pairs={{0,2},{2,0},{1,3},{3,1},{4,6},{6,4},{5,7},{7,5},{8,10},{10,8},{9,1... | collective-permute-start | bytes 12296 | tf_op jit(solution)/shard_map/ppermute | solution.py:47
  271.7 5.2 collective-permute-start.16
  276.9 5.4 collective-permute-start.12
  277.3 16.1 %collective-permute-start.21 = (bf16[2,2,2,1,256]{4,2,1,0,3:T(2,128)(2,1)S(1)}, bf16[2,2,2,1,256]{4,2,1,0,3:T(2,128)(2,1)S(1)}, u32[]{:S(2)}, u32[]{:S(2)}) collective-permute-start(bf16[2,2,2,1,256]{4,2,1,0,3:T(2,128)(2,1)S(1)} %get-tuple-element.293), channel_id=1, source_target_pairs={{0,1},{1,0},{2,3},{3,2},{4,5},{5,4},{6,7},{7,6},{8,9},{9,8},{10,11... | collective-permute-start | bytes 12296 | tf_op jit(solution)/shard_map/ppermute | solution.py:47
  282.3 11.9 %collective-permute-start.17 = (bf16[2,2,2,1,256]{4,2,1,0,3:T(2,128)(2,1)S(1)}, bf16[2,2,2,1,256]{4,2,1,0,3:T(2,128)(2,1)S(1)}, u32[]{:S(2)}, u32[]{:S(2)}) collective-permute-start(bf16[2,2,2,1,256]{4,2,1,0,3:T(2,128)(2,1)S(1)} %broadcast_select_fusion.46), channel_id=1, source_target_pairs={{0,1},{1,0},{2,3},{3,2},{4,5},{5,4},{6,7},{7,6},{8,9},{9,8},{10,11... | collective-permute-start | bytes 12296 | tf_op jit(solution)/shard_map/ppermute | solution.py:47
  286.0 6.5 %collective-permute-start.27 = (bf16[2,1,1024,64]{2,3,0,1:T(8,128)(2,1)S(1)}, bf16[2,1,1024,64]{2,3,0,1:T(8,128)(2,1)S(1)}, u32[]{:S(2)}, u32[]{:S(2)}) collective-permute-start(bf16[2,1,1024,64]{2,3,0,1:T(8,128)(2,1)S(1)} %bitcast_select_fusion.9), channel_id=1, source_target_pairs={{0,4},{4,0},{1,5},{5,1},{2,6},{6,2},{3,7},{7,3},{8,12},{12,8},{9,1... | collective-permute-start | bytes 786440 | tf_op jit(solution)/shard_map/ppermute | solution.py:47
  292.4 3.6 collective-permute-start.13
  293.3 8.1 %collective-permute-start.28 = (bf16[2,2,1,512,64]{3,4,0,1,2:T(8,128)(2,1)}, bf16[2,2,1,512,64]{3,4,0,1,2:T(8,128)(2,1)S(1)}, u32[]{:S(2)}, u32[]{:S(2)}) collective-permute-start(bf16[2,2,1,512,64]{3,4,0,1,2:T(8,128)(2,1)} %copy_select_fusion), channel_id=1, source_target_pairs={{0,2},{2,0},{1,3},{3,1},{4,6},{6,4},{5,7},{7,5},{8,10},{10,8},{9,1... | collective-permute-start | bytes 786440 | tf_op jit(solution)/shard_map/ppermute | solution.py:47
  301.7 193.7 %collective-permute-start.29 = (bf16[2,2,2,1,256,64]{4,5,2,1,0,3:T(8,128)(2,1)S(1)}, bf16[2,2,2,1,256,64]{4,5,2,1,0,3:T(8,128)(2,1)S(1)}, u32[]{:S(2)}, u32[]{:S(2)}) collective-permute-start(bf16[2,2,2,1,256,64]{4,5,2,1,0,3:T(8,128)(2,1)S(1)} %bitcast_select_fusion.8), channel_id=1, source_target_pairs={{0,1},{1,0},{2,3},{3,2},{4,5},{5,4},{6,7},{7,6},{8,9},{9,8},{10,11... | collective-permute-start | bytes 786440 | tf_op jit(solution)/shard_map/ppermute | solution.py:47
  (26 other events, 127.0 us)
Sparse Core Ops, SparseCore 0:
  92.5 163.9 all-gather.2
where the time goes:
time: 625 us; the launch traced here: 616 us
  matrix products  215 us (34%)
  local copies, waits for them, and re-layouts  171 us (27%)
  other arithmetic  88.9 us (14%)
  waiting for transfers between devices  63.7 us (10%)
  starting transfers between devices  61.9 us (10%)
  between operations  14.9 us (2%)
    dot_general x33, matrix products, attend_one(): jnp.einsum('qk,kd->qd', powers.astype(jnp.bfloat16), values, preferred_el...  134 us
    dot_general x33, matrix products, attend_one(): jnp.einsum('qd,kd->qk', query, keys, preferred_element_type=jnp.float32)  81.1 us
    ppermute x30, waiting for transfers between devices, partner(): return lax.ppermute(block, axis, route)  63.7 us
    ppermute x30, starting transfers between devices, partner(): return lax.ppermute(block, axis, route)  61.8 us
    reduce_sum x33, other arithmetic, attend_one(): total = jnp.sum(powers, axis=-1, keepdims=True)  55.9 us
    reshape x6, local copies, waits for them, and re-layouts, dilate_tokens(): array.reshape(heads, length // rate, rate, depth)  35.8 us
    transpose x5, local copies, waits for them, and re-layouts, to_heads(): return array.reshape(length, H, HD).transpose(1, 0, 2)  25.4 us
    while x32, local copies, waits for them, and re-layouts  22 us
  transfers between devices with their start and end apart: 31, of which 15 were waited for; matrix products, arithmetic and copies ran while one was open for 56% of the time, Pallas kernels for 0%

commit v1 on v0

v1 whole, which is shorter than its diff:
```python
import functools

import jax
import jax.numpy as jnp
import numpy as np
from jax import lax
from jax.experimental import pallas as pl
from jax.experimental.pallas import tpu as pltpu
from jax.sharding import PartitionSpec as P


F32 = jnp.float32
BF = jnp.bfloat16
SCALE = float(np.log2(np.e) / 8.0)
PAIRS = 8
TOK = 1024
MID = 256
FAR = 32
CHUNKS = ((0, 2), (2, 2), (4, 2), (6, 1), (7, 1))
RET = 160
VMEM = 56 * 2**20


def params(axes):
    return pltpu.CompilerParams(dimension_semantics=("arbitrary",) * axes, vmem_limit_bytes=VMEM)


def token_class(slot, head):
    a, b = slot // 8, slot % 8
    return 4 * ((b + head // 4) % 8) + (a + head) % 4


def order_matrix(by_class):
    a = lax.broadcasted_iota(jnp.int32, (256, 256), 0)
    b = lax.broadcasted_iota(jnp.int32, (256, 256), 1)
    if not by_class:
        a, b = b, a
    return (b == 32 * (a % 8) + a // 8).astype(F32).astype(BF)


def prep_kernel(q_ref, k_ref, v_ref, qf_ref, qkvm_ref, kvm_ref, kvr_ref, *rest):
    sent, wide = rest[:-1], rest[-1]
    step = pl.program_id(0)
    order = order_matrix(True)
    low = lax.broadcasted_iota(jnp.int32, (8, 128), 1) < 64
    for n, ref in enumerate((q_ref, k_ref, v_ref)):
        for t in range(4):
            block = ref[t * 256 : (t + 1) * 256, :]
            wide[n, t] = jnp.dot(order, block, preferred_element_type=F32)
    for pair in range(2):
        g = 2 * step + pair
        lanes = slice(pair * 128, (pair + 1) * 128)
        for slot in range(32):
            c0 = pl.multiple_of(token_class(slot, 2 * g) * 8, 8)
            c1 = pl.multiple_of(token_class(slot, 2 * g + 1) * 8, 8)
            row = slot * FAR
            for n in range(3):
                x = jnp.concatenate(
                    [
                        jnp.where(low, wide[n, t, pl.ds(c0, 8), lanes], wide[n, t, pl.ds(c1, 8), lanes])
                        for t in range(4)
                    ],
                    axis=0,
                ).astype(BF)
                if n == 0:
                    qf_ref[pair, row : row + FAR, :] = x
                elif slot < 8:
                    kvm_ref[pair, n - 1, row : row + FAR, :] = x
                else:
                    kvr_ref[pair, n - 1, row - MID : row - MID + FAR, :] = x
                if slot < 8:
                    qkvm_ref[pair, n, row : row + FAR, :] = x
    for (first, count), out in zip(CHUNKS, sent):

        @pl.when(step == first // 2)
        def _():
            out[...] = kvr_ref[first % 2 : first % 2 + count]


def prep(q, k, v):
    col = pl.BlockSpec((TOK, 256), lambda g: (0, g))
    return pl.pallas_call(
        prep_kernel,
        grid=(PAIRS // 2,),
        in_specs=[col, col, col],
        out_specs=[
            pl.BlockSpec((2, TOK, 128), lambda g: (g, 0, 0)),
            pl.BlockSpec((2, 3, MID, 128), lambda g: (g, 0, 0, 0)),
            pl.BlockSpec((2, 2, MID, 128), lambda g: (g, 0, 0, 0)),
            pl.BlockSpec((2, 2, TOK - MID, 128), lambda g: (g, 0, 0, 0)),
        ]
        + [pl.BlockSpec((n, 2, TOK - MID, 128), lambda g: (0, 0, 0, 0)) for _, n in CHUNKS],
        out_shape=[
            jax.ShapeDtypeStruct((PAIRS, TOK, 128), BF),
            jax.ShapeDtypeStruct((PAIRS, 3, MID, 128), BF),
            jax.ShapeDtypeStruct((PAIRS, 2, MID, 128), BF),
            jax.ShapeDtypeStruct((PAIRS, 2, TOK - MID, 128), BF),
        ]
        + [jax.ShapeDtypeStruct((n, 2, TOK - MID, 128), BF) for _, n in CHUNKS],
        scratch_shapes=[pltpu.VMEM((3, 4, 256, 256), F32)],
        compiler_params=params(1),
        name="prep",
    )(q, k, v)


def rows_of(refs):
    parts = [r[...].reshape(-1, 128) for r in refs]
    return parts[0] if len(parts) == 1 else jnp.concatenate(parts, axis=0)


def scaled_query(q, head):
    lane = lax.broadcasted_iota(jnp.int32, q.shape, 1)
    own = (lane >= 64) == (head == 1)
    q = q.astype(F32) * SCALE
    hi = q.astype(BF)
    lo = (q - hi.astype(F32)).astype(BF)
    zero = jnp.zeros_like(hi)
    return jnp.concatenate([jnp.where(own, hi, zero), jnp.where(own, lo, zero)], axis=1)


def score(keys, query):
    both = jnp.concatenate([keys, keys], axis=1)
    return lax.dot_general(both, query, (((1,), (1,)), ((), ())), preferred_element_type=F32)


def set_values(vt, v):
    t = v.T
    for e in range(2):
        vt[e, 0:64, :] = t[e * 64 : (e + 1) * 64, :]
        vt[e, 64:80, :] = jnp.ones((16, t.shape[1]), BF)


def mix(vt, p):
    return lax.dot_general(vt, p, (((1,), (0,)), ((), ())), preferred_element_type=F32)


def attend_kernel(*refs, parts, carried, qb, qt):
    q_ref, refs = refs[0], refs[1:]
    k_refs, v_refs, refs = refs[:parts], refs[parts : 2 * parts], refs[2 * parts :]
    if carried:
        oi_ref, mi_ref, refs = refs[0], refs[1], refs[2:]
    o_ref, m_ref, vt = refs

    @pl.when(pl.program_id(1) == 0)
    def _():
        set_values(vt, rows_of(v_refs))

    queries = q_ref[...].reshape(qb, 128)
    keys = rows_of(k_refs)
    safe = jnp.ones((1, qt), F32)
    for t in range(qb // qt):
        cols = slice(t * qt, (t + 1) * qt)
        for e in range(2):
            s = score(keys, scaled_query(queries[t * qt : (t + 1) * qt], e))
            a = mix(vt[e], jnp.exp2(s).astype(BF))
            o, den = a[:64], a[64:65]
            if carried:
                o = o + oi_ref[0, e * 64 : (e + 1) * 64, cols]
                den = den + mi_ref[0, 2 * e + 1, :, cols]
                safe = jnp.where(mi_ref[0, 2 * e, :, cols] == 0.0, safe, 0.0)
            safe = jnp.where((den > 2.0**-80) & (den < 2.0**120), safe, 0.0)
            o_ref[0, e * 64 : (e + 1) * 64, cols] = o
            m_ref[0, 2 * e, :, cols] = jnp.zeros((1, qt), F32)
            m_ref[0, 2 * e + 1, :, cols] = den

    @pl.when(jnp.min(safe) < 0.5)
    def _():
        def shifted(n, carry):
            e = n % 2
            cols = pl.ds(pl.multiple_of((n // 2) * 256, 256), 256)
            heads = pl.ds(pl.multiple_of(e * 64, 64), 64)
            if len(q_ref.shape) == 3:
                q = q_ref[0, cols, :]
            else:
                q = q_ref[n // 2, 0]
            s = score(rows_of(k_refs), scaled_query(q, e))
            peak = jnp.max(s, axis=0, keepdims=True)
            if carried:
                peak = jnp.maximum(peak, mi_ref[0, 2 * e, :, cols])
            a = mix(vt[e], jnp.exp2(s - peak).astype(BF))
            o, den = a[:64], a[64:65]
            if carried:
                w = jnp.exp2(mi_ref[0, 2 * e, :, cols] - peak)
                o = o + w * oi_ref[0, heads, cols]
                den = den + w * mi_ref[0, 2 * e + 1, :, cols]
            o_ref[0, heads, cols] = o
            m_ref[0, 2 * e, :, cols] = peak
            m_ref[0, 2 * e + 1, :, cols] = den
            return carry

        lax.fori_loop(0, 2 * (qb // 256), shifted, 0)


def attend(groups, nq, qb, qt, query, parts, carry=None, carry_first=0):
    nk = sum(p[3] for p in parts)
    specs = [query[1]] + [p[1] for p in parts] + [p[2] for p in parts]
    args = [query[0]] + [p[0] for p in parts] + [p[0] for p in parts]

    def carry_specs(first):
        return [
            pl.BlockSpec((1, 128, qb), lambda g, j: (g + first, 0, j)),
            pl.BlockSpec((1, 4, 1, qb), lambda g, j: (g + first, 0, 0, j)),
        ]

    if carry is not None:
        specs += carry_specs(carry_first)
        args += list(carry)
    exps = groups * 2 * nq * nk
    return pl.pallas_call(
        functools.partial(
            attend_kernel, parts=len(parts), carried=carry is not None, qb=qb, qt=qt
        ),
        grid=(groups, nq // qb),
        in_specs=specs,
        out_specs=carry_specs(0),
        out_shape=[
            jax.ShapeDtypeStruct((groups, 128, nq), F32),
            jax.ShapeDtypeStruct((groups, 4, 1, nq), F32),
        ],
        scratch_shapes=[pltpu.VMEM((2, 80, nk), BF)],
        compiler_params=params(2),
        cost_estimate=pl.CostEstimate(
            flops=exps * 1100, bytes_accessed=groups * (nq + nk) * 1024, transcendentals=exps
        ),
    )(*args)


def near(first, count, qf, kvm, kvr, kvr_first, carry=None, carry_first=0):
    def part(array, base, rows):
        return (
            array,
            pl.BlockSpec((1, 1, rows, 128), lambda g, j: (g + base, 0, 0, 0)),
            pl.BlockSpec((1, 1, rows, 128), lambda g, j: (g + base, 1, 0, 0)),
            rows,
        )

    return attend(
        count,
        TOK,
        TOK,
        1024,
        (qf, pl.BlockSpec((1, TOK, 128), lambda g, j: (g + first, j, 0))),
        [part(kvm, first, MID), part(kvr, kvr_first, TOK - MID)],
        carry,
        carry_first,
    )


def middle(own, keys, at, carry=None):
    nq = PAIRS * MID
    qb = 1024
    return attend(
        1,
        nq,
        qb,
        512,
        (own, pl.BlockSpec((qb // MID, 1, MID, 128), lambda g, j: (j, 0, 0, 0))),
        [
            (
                keys,
                pl.BlockSpec((PAIRS, 1, MID, 128), lambda g, j: (0, at, 0, 0)),
                pl.BlockSpec((PAIRS, 1, MID, 128), lambda g, j: (0, at + 1, 0, 0)),
                PAIRS * MID,
            )
        ],
        carry,
    )


def far_kernel(q_ref, ka, kb, kc, va, vb, vc, o_ref, m_ref, ret_ref, vt):
    set_values(vt, rows_of((va, vb, vc)))
    keys = rows_of((ka, kb, kc))
    queries = rows_of((q_ref,))
    outs, levels = [], []
    for e in range(2):
        s = score(keys, scaled_query(queries, e))
        peak = jnp.max(s, axis=0, keepdims=True)
        a = mix(vt[e], jnp.exp2(s - peak).astype(BF))
        outs.append(a[:64] / a[64:65])
        levels.append(peak + jnp.log2(a[64:65]))
    row = lax.broadcasted_iota(jnp.int32, (16, MID), 0)
    first = lax.broadcasted_iota(jnp.int32, (1, MID), 1) < FAR
    for d in range(PAIRS):
        cols = slice(d * MID, (d + 1) * MID)
        lev = jnp.zeros((16, MID), F32)
        for e in range(2):
            heads = slice(e * 64, (e + 1) * 64)
            peak = m_ref[0, 2 * e, :, cols]
            den = m_ref[0, 2 * e + 1, :, cols]
            o = o_ref[0, heads, cols]
            fo = outs[e][:, d * FAR : (d + 1) * FAR]
            fl = levels[e][:, d * FAR : (d + 1) * FAR]
            fo = jnp.concatenate([fo, jnp.zeros((64, MID - FAR), F32)], axis=1)
            fl = jnp.concatenate([fl, jnp.zeros((1, MID - FAR), F32)], axis=1)
            fl = jnp.where(first, fl, -1e30)
            top = jnp.maximum(peak, fl)
            wm = jnp.exp2(peak - top)
            wf = jnp.exp2(fl - top)
            total = wm * den + wf
            ret_ref[d, heads, :] = ((wm * o + wf * fo) / total).astype(BF)
            level = top + jnp.log2(total)
            for part in range(3):
                piece = level.astype(BF).astype(F32)
                level = level - piece
                lev = jnp.where(row == 3 * e + part, piece, lev)
        ret_ref[d, 128:144, :] = lev.astype(BF)
        ret_ref[d, 144:160, :] = jnp.concatenate(
            [
                outs[b // 4][16 * (b % 4) : 16 * (b % 4) + 16, d * FAR : (d + 1) * FAR]
                for b in range(8)
            ],
            axis=1,
        ).astype(BF)


def far_and_return(own, partner, other, mid):
    def part(lead, at):
        return pl.BlockSpec((lead, 1, FAR, 128), lambda i: (0, at, 0, 0))

    whole = lambda i: (0, 0, 0)
    return pl.pallas_call(
        far_kernel,
        grid=(1,),
        in_specs=[
            part(PAIRS, 0),
            part(PAIRS, 1),
            part(PAIRS, 0),
            part(2 * PAIRS, 0),
            part(PAIRS, 2),
            part(PAIRS, 1),
            part(2 * PAIRS, 1),
            pl.BlockSpec((1, 128, PAIRS * MID), whole),
            pl.BlockSpec((1, 4, 1, PAIRS * MID), lambda i: (0, 0, 0, 0)),
        ],
        out_specs=pl.BlockSpec((PAIRS, RET, MID), whole),
        out_shape=jax.ShapeDtypeStruct((PAIRS, RET, MID), BF),
        scratch_shapes=[pltpu.VMEM((2, 80, 1024), BF)],
        compiler_params=params(1),
        name="far",
    )(own, own, partner, other, own, partner, other, *mid)


def merge_kernel(o_ref, m_ref, ret_ref, *rest, first):
    out_ref, turned = rest[-2:]
    g = pl.program_id(0) + first
    parts = []
    lev = ret_ref[0, 128:144, :].astype(F32)
    for e in range(2):
        heads = slice(e * 64, (e + 1) * 64)
        peak = m_ref[0, 2 * e, :, :MID]
        den = m_ref[0, 2 * e + 1, :, :MID]
        level = lev[3 * e : 3 * e + 1] + lev[3 * e + 1 : 3 * e + 2] + lev[3 * e + 2 : 3 * e + 3]
        top = jnp.maximum(peak, level)
        wn = jnp.exp2(peak - top)
        wm = jnp.exp2(level - top)
        inv = 1.0 / (wn * den + wm)
        head = (wn * inv) * o_ref[0, heads, :MID] + (wm * inv) * ret_ref[0, heads, :].astype(F32)
        tail = o_ref[0, heads, MID:] * (1.0 / m_ref[0, 2 * e + 1, :, MID:])
        parts.append(jnp.concatenate([head, tail], axis=1))
    turned[...] = jnp.concatenate(parts, axis=0).T
    order = order_matrix(False)
    low = lax.broadcasted_iota(jnp.int32, (8, 128), 1) < 64
    starts = []
    for cls in range(32):
        for e in range(2):
            h = 2 * g + e
            a = (cls % 4 - h + 16) % 4
            b = (cls // 4 - h // 4 + 8) % 8
            starts.append(a * 256 + b * 32)
    for t in range(4):
        rows = []
        for cls in range(32):
            r0 = pl.multiple_of(starts[2 * cls] + 8 * t, 8)
            r1 = pl.multiple_of(starts[2 * cls + 1] + 8 * t, 8)
            rows.append(jnp.where(low, turned[pl.ds(r0, 8), :], turned[pl.ds(r1, 8), :]))
        block = jnp.concatenate(rows, axis=0).astype(BF)
        out_ref[t * 256 : (t + 1) * 256, :] = jnp.dot(
            order, block, preferred_element_type=F32
        ).astype(BF)


def merge(first, count, carry, ret, out):
    specs = [
        pl.BlockSpec((1, 128, TOK), lambda g: (g, 0, 0)),
        pl.BlockSpec((1, 4, 1, TOK), lambda g: (g, 0, 0, 0)),
        pl.BlockSpec((1, RET, MID), lambda g: (g + first, 0, 0)),
    ]
    args = [*carry, ret]
    alias = {}
    if out is not None:
        specs.append(pl.BlockSpec(memory_space=pl.ANY))
        args.append(out)
        alias = {3: 0}
    return pl.pallas_call(
        functools.partial(merge_kernel, first=first),
        grid=(count,),
        in_specs=specs,
        out_specs=pl.BlockSpec((TOK, 128), lambda g: (0, g + first)),
        out_shape=jax.ShapeDtypeStruct((TOK, PAIRS * 128), BF),
        scratch_shapes=[pltpu.VMEM((TOK, 128), F32)],
        input_output_aliases=alias,
        compiler_params=params(1),
        name="merge",
    )(*args)


GROUPS = [
    [y * 16 + x * 4 + z for x in range(4) for z in pair] for y in range(2) for pair in ((1, 2), (0, 3))
]
NEAR = [(i, i ^ 1) for i in range(32)]
PLANE = [(i, i ^ 16) for i in range(32)]


def exchange(x):
    return lax.all_to_all(x, "seq", 0, 0, axis_index_groups=GROUPS, tiled=True)


def steps(queries, keys, values):
    qf, qkvm, kvm, kvr, *sent = prep(queries, keys, values)
    kvm_there = lax.ppermute(kvm, "seq", NEAR)
    own = exchange(qkvm)
    kvr_there = []
    for part in sent:
        kvr_there.append(lax.ppermute(part, "seq", NEAR))
    partner = exchange(kvm_there)
    half = PAIRS // 2
    here = []
    for i in range(2):
        here.append(near(i * half, half, qf, kvm, kvr, i * half))
    far_kv = jnp.concatenate([own[:, 1:, :FAR], partner[:, :, :FAR]], axis=0)
    other = lax.ppermute(far_kv, "seq", PLANE)
    mid = middle(own, own, 1)
    mid = middle(own, partner, 0, mid)
    ret = far_and_return(own, partner, other, mid)
    ret = exchange(ret)
    far_rows = ret[:, 144:, :].reshape(PAIRS, 16, 8, FAR).transpose(3, 0, 2, 1).reshape(FAR, PAIRS * 128)
    out = None
    for i, (a, n) in enumerate(CHUNKS):
        both = near(a, n, qf, kvm_there, kvr_there[i], 0, here[a // half], a % half)
        out = merge(a, n, both, ret, out)
    return out, far_rows


def solution(mesh):
    spec = P(("dp", "seq"), None)
    return jax.shard_map(
        steps, mesh=mesh, in_specs=(spec, spec, spec), out_specs=(spec, spec), check_vma=False
    )
```

time: 625 us -> 274 us (0.44)
  the two profiles are of different devices: /device:TPU:56 before, /device:TPU:2 now
where the time goes in v1:
time: 274 us; the launch traced here: 273 us
  Pallas kernels  238 us (87%)
  starting transfers between devices  30.5 us (11%)
  local copies, waits for them, and re-layouts  3.55 us (1%)
    pallas_call x9, Pallas kernels, attend(): pl.pallas_call(functools.partial(attend_kernel, parts=len(parts), carried...  211 us
    all_to_all x3, starting transfers between devices, exchange(): return lax.all_to_all(x, 'seq', 0, 0, axis_index_groups=GROUPS, tiled=True)  22.3 us
    pallas_call x5, Pallas kernels, merge(): pl.pallas_call(functools.partial(merge_kernel, first=first), grid=(count,...  13 us
    pallas_call x1, Pallas kernels, prep(): pl.pallas_call(prep_kernel, grid=(PAIRS // 2,), in_specs=[col, col, col],...  10.3 us
    ppermute x5, starting transfers between devices, steps(): kvr_there.append(lax.ppermute(part, 'seq', NEAR))  6.31 us
  transfers between devices with their start and end apart: 10, of which 0 were waited for; matrix products, arithmetic and copies ran while one was open for 0% of the time, Pallas kernels for 79%

profile of v1, /device:TPU:2, one launch (start us, length us, event | category | flops | bytes accessed | tf_op | source)
XLA Modules:
  0.0 273.2 jit_solution(6241016969401624656)
XLA Ops:
  0.6 10.3 %prep.1 = (bf16[8,1024,128]{2,1,0:T(8,128)(2,1)}, bf16[8,3,256,128]{3,2,1,0:T(8,128)(2,1)}, bf16[8,2,256,128]{3,2,1,0:T(8,128)(2,1)}, bf16[8,2,768,128]{3,2,1,0:...) custom-call(bf16[1024,1024]{1,0:T(8,128)(2,1)} %q_ref.1, ...), custom_call_target="tpu_custom_call" | custom-call | tf_op jit(solution)/shard_map/prep/pallas_call | solution.py:82
  10.9 8.4 %all-to-all-start = ((bf16[8,3,256,128]{3,2,1,0:T(8,128)(2,1)}), bf16[8,3,256,128]{3,2,1,0:T(8,128)(2,1)S(1)}, u32[]{:S(2)}, u32[]{:S(2)}) async-start(bf16[8,3,256,128]{3,2,1,0:T(8,128)(2,1)} %get-tuple-element.37), calls=%async_computation | async-start | bytes 3145728 | tf_op jit(solution)/shard_map/all_to_all | solution.py:415
  19.4 0.0 collective-permute-start.1
  19.4 2.0 collective-permute-start.3
  21.4 0.0 collective-permute-start.4
  21.5 2.0 collective-permute-start.6
  23.5 0.0 collective-permute-start
  23.5 35.6 %shard_map.56 = (f32[4,128,1024]{2,1,0:T(8,128)}, f32[4,4,1,1024]{3,2,1,0:T(1,128)}) custom-call(bf16[8,1024,128]{2,1,0:T(8,128)(2,1)} %get-tuple-element.29.refs_0_, bf16[8,2,256,128]{3,2,1,0:T(8,128)(2,1)} %get-tuple-element.30.refs_1_.refs_3_, bf16[8,2,768,128]{3,2,1,0:T(8,128)(2,1)} %get-tuple-element.32.refs_2_.refs_4_, ...), custom_call_target="tpu_custom_call" | custom-call | flops 9227468800 | bytes 8388608 | tf_op jit(solution)/shard_map/pallas_call | solution.py:209
  59.1 35.7 %shard_map.50 = (f32[4,128,1024]{2,1,0:T(8,128)}, f32[4,4,1,1024]{3,2,1,0:T(1,128)}) custom-call(bf16[8,1024,128]{2,1,0:T(8,128)(2,1)} %get-tuple-element.29.refs_0_, bf16[8,2,256,128]{3,2,1,0:T(8,128)(2,1)} %get-tuple-element.30.refs_1_.refs_3_, bf16[8,2,768,128]{3,2,1,0:T(8,128)(2,1)} %get-tuple-element.32.refs_2_.refs_4_, ...), custom_call_target="tpu_custom_call" | custom-call | flops 9227468800 | bytes 8388608 | tf_op jit(solution)/shard_map/pallas_call | solution.py:209
  94.8 0.0 collective-permute-done.4.refs_2_.refs_4_
  94.9 2.3 collective-permute-start.5
  97.1 1.0 copy-done.4
  98.1 19.0 %shard_map.55 = (f32[2,128,1024]{2,1,0:T(8,128)}, f32[2,4,1,1024]{3,2,1,0:T(1,128)}) custom-call(bf16[8,1024,128]{2,1,0:T(8,128)(2,1)} %get-tuple-element.29.refs_0_, bf16[8,2,256,128]{3,2,1,0:T(8,128)(2,1)} %copy-done.4, bf16[2,2,768,128]{3,2,1,0:T(8,128)(2,1)} %copy-done.8, bf16[8,2,256,128]{3,2,1,0:T(8,128)(2,1)} %copy-done.4, ...), custom_call_target="tpu_custom_call" | custom-call | flops 4613734400 | bytes 4194304 | tf_op jit(solution)/shard_map/pallas_call | solution.py:209
  117.1 0.9 copy-done.7
  118.0 19.0 %shard_map.58 = (f32[2,128,1024]{2,1,0:T(8,128)}, f32[2,4,1,1024]{3,2,1,0:T(1,128)}) custom-call(bf16[8,1024,128]{2,1,0:T(8,128)(2,1)} %get-tuple-element.29.refs_0_, bf16[8,2,256,128]{3,2,1,0:T(8,128)(2,1)} %copy-done.4, bf16[2,2,768,128]{3,2,1,0:T(8,128)(2,1)} %copy-done.7, bf16[8,2,256,128]{3,2,1,0:T(8,128)(2,1)} %copy-done.4, ...), custom_call_target="tpu_custom_call" | custom-call | flops 4613734400 | bytes 4194304 | tf_op jit(solution)/shard_map/pallas_call | solution.py:209
  137.0 6.9 %all-to-all-start.1 = ((bf16[8,2,256,128]{3,2,1,0:T(8,128)(2,1)}), bf16[8,2,256,128]{3,2,1,0:T(8,128)(2,1)S(1)}, u32[]{:S(2)}, u32[]{:S(2)}) async-start(bf16[8,2,256,128]{3,2,1,0:T(8,128)(2,1)} %copy-done.4), calls=%async_computation.1 | async-start | bytes 2097152 | tf_op jit(solution)/shard_map/all_to_all | solution.py:415
  144.0 10.5 %shard_map.54 = (f32[1,128,1024]{2,1,0:T(8,128)}, f32[1,4,1,1024]{3,2,1,0:T(1,128)}) custom-call(bf16[8,1024,128]{2,1,0:T(8,128)(2,1)} %get-tuple-element.29.refs_0_, bf16[8,2,256,128]{3,2,1,0:T(8,128)(2,1)} %copy-done.4, bf16[1,2,768,128]{3,2,1,0:T(8,128)(2,1)} %collective-permute-done.3.refs_2_.refs_4_, bf16[8,2,256,128]{3,2,1,0:T(8,128)(2,1)} %copy-done.4, ...), custom_call_target="tpu_custom_call" | custom-call | flops 2306867200 | bytes 2097152 | tf_op jit(solution)/shard_map/pallas_call | solution.py:209
  154.5 30.5 %shard_map.52 = (f32[1,128,2048]{2,1,0:T(8,128)}, f32[1,4,1,2048]{3,2,1,0:T(1,128)}) custom-call(bf16[8,3,256,128]{3,2,1,0:T(8,128)(2,1)} %copy-done, bf16[8,3,256,128]{3,2,1,0:T(8,128)(2,1)} %copy-done, bf16[8,3,256,128]{3,2,1,0:T(8,128)(2,1)} %copy-done), custom_call_target="tpu_custom_call" | custom-call | flops 9227468800 | bytes 4194304 | tf_op jit(solution)/shard_map/pallas_call | solution.py:209
  185.0 1.9 collective-permute-start.2
  186.9 30.7 %shard_map.53 = (f32[1,128,2048]{2,1,0:T(8,128)}, f32[1,4,1,2048]{3,2,1,0:T(1,128)}) custom-call(bf16[8,3,256,128]{3,2,1,0:T(8,128)(2,1)} %copy-done, bf16[8,2,256,128]{3,2,1,0:T(8,128)(2,1)} %copy-done.2, bf16[8,2,256,128]{3,2,1,0:T(8,128)(2,1)} %copy-done.2, f32[1,128,2048]{2,1,0:T(8,128)} %get-tuple-element.38.refs_3_, ...), custom_call_target="tpu_custom_call" | custom-call | flops 9227468800 | bytes 4194304 | tf_op jit(solution)/shard_map/pallas_call | solution.py:209
  217.6 0.7 copy-done.3
  218.3 4.1 %far.1 = bf16[8,160,256]{2,1,0:T(8,128)(2,1)} custom-call(bf16[8,3,256,128]{3,2,1,0:T(8,128)(2,1)} %copy-done, bf16[8,3,256,128]{3,2,1,0:T(8,128)(2,1)} %copy-done, bf16[8,2,256,128]{3,2,1,0:T(8,128)(2,1)} %copy-done.2, bf16[16,2,32,128]{3,2,1,0:T(8,128)(2,1)} %copy-done.3, bf16[8,3,256,128]{3,2,1,0:T(8,128)(2,1)} %copy-done, ...), custom_call_target="tpu_custom_call" | custom-call | tf_op jit(solution)/shard_map/far/pallas_call | solution.py:321
  222.4 6.9 %all-to-all-start.2 = ((bf16[8,160,256]{2,1,0:T(8,128)(2,1)}), bf16[8,160,256]{2,1,0:T(8,128)(2,1)S(1)}, u32[]{:S(2)}, u32[]{:S(2)}) async-start(bf16[8,160,256]{2,1,0:T(8,128)(2,1)} %far.1), calls=%async_computation.2 | async-start | bytes 1310720 | tf_op jit(solution)/shard_map/all_to_all | solution.py:415
  229.4 10.8 %shard_map.51 = (f32[1,128,1024]{2,1,0:T(8,128)}, f32[1,4,1,1024]{3,2,1,0:T(1,128)}) custom-call(bf16[8,1024,128]{2,1,0:T(8,128)(2,1)} %get-tuple-element.29.refs_0_, bf16[8,2,256,128]{3,2,1,0:T(8,128)(2,1)} %copy-done.4, bf16[1,2,768,128]{3,2,1,0:T(8,128)(2,1)} %collective-permute-done.1.refs_2_.refs_4_, bf16[8,2,256,128]{3,2,1,0:T(8,128)(2,1)} %copy-done.4, ...), custom_call_target="tpu_custom_call" | custom-call | flops 2306867200 | bytes 2097152 | tf_op jit(solution)/shard_map/pallas_call | solution.py:209
  240.1 19.0 %shard_map.57 = (f32[2,128,1024]{2,1,0:T(8,128)}, f32[2,4,1,1024]{3,2,1,0:T(1,128)}) custom-call(bf16[8,1024,128]{2,1,0:T(8,128)(2,1)} %get-tuple-element.29.refs_0_, bf16[8,2,256,128]{3,2,1,0:T(8,128)(2,1)} %copy-done.4, bf16[2,2,768,128]{3,2,1,0:T(8,128)(2,1)} %collective-permute-done.5.refs_2_.refs_4_, bf16[8,2,256,128]{3,2,1,0:T(8,128)(2,1)} %copy-done.4, ...), custom_call_target="tpu_custom_call" | custom-call | flops 4613734400 | bytes 4194304 | tf_op jit(solution)/shard_map/pallas_call | solution.py:209
  259.2 0.2 reshape.10
  259.4 0.8 copy.11
  260.2 2.9 %merge.5.rest_0_ = bf16[1024,1024]{1,0:T(8,128)(2,1)} custom-call(f32[2,128,1024]{2,1,0:T(8,128)} %get-tuple-element.54.o_ref, f32[2,4,1,1024]{3,2,1,0:T(1,128)} %get-tuple-element.55.m_ref, bf16[8,160,256]{2,1,0:T(8,128)(2,1)} %copy-done.1), custom_call_target="tpu_custom_call" | custom-call | tf_op jit(solution)/shard_map/merge/pallas_call | solution.py:394
  263.1 2.9 %merge.6.rest_0_ = bf16[1024,1024]{1,0:T(8,128)(2,1)} custom-call(f32[2,128,1024]{2,1,0:T(8,128)} %get-tuple-element.51.o_ref, f32[2,4,1,1024]{3,2,1,0:T(1,128)} %get-tuple-element.52.m_ref, bf16[8,160,256]{2,1,0:T(8,128)(2,1)} %copy-done.1, bf16[1024,1024]{1,0:T(8,128)(2,1)} %merge.5.rest_0_), custom_call_target="tpu_custom_call", output_to_operand_aliasing={{}: (3, {})} | custom-call | tf_op jit(solution)/shard_map/merge/pallas_call | solution.py:394
  265.9 2.9 %merge.7.rest_0_ = bf16[1024,1024]{1,0:T(8,128)(2,1)} custom-call(f32[2,128,1024]{2,1,0:T(8,128)} %get-tuple-element.46.o_ref, f32[2,4,1,1024]{3,2,1,0:T(1,128)} %get-tuple-element.47.m_ref, bf16[8,160,256]{2,1,0:T(8,128)(2,1)} %copy-done.1, bf16[1024,1024]{1,0:T(8,128)(2,1)} %merge.6.rest_0_), custom_call_target="tpu_custom_call", output_to_operand_aliasing={{}: (3, {})} | custom-call | tf_op jit(solution)/shard_map/merge/pallas_call | solution.py:394
  268.8 2.2 merge.8.rest_0_
  271.0 2.2 merge.9
  (29 shorter events, 0.1 us)
Async XLA Ops:
  10.9 12.5 %copy-start.5 = (bf16[8,2,256,128]{3,2,1,0:T(8,128)(2,1)S(1)}, bf16[8,2,256,128]{3,2,1,0:T(8,128)(2,1)}, u32[]{:S(2)}) copy-start(bf16[8,2,256,128]{3,2,1,0:T(8,128)(2,1)} %get-tuple-element.30.refs_1_.refs_3_) | copy-start | bytes 3145732
  10.9 126.1 %all-to-all-start = ((bf16[8,3,256,128]{3,2,1,0:T(8,128)(2,1)}), bf16[8,3,256,128]{3,2,1,0:T(8,128)(2,1)S(1)}, u32[]{:S(2)}, u32[]{:S(2)}) async-start(bf16[8,3,256,128]{3,2,1,0:T(8,128)(2,1)} %get-tuple-element.37), calls=%async_computation | async-start | bytes 3145728 | tf_op jit(solution)/shard_map/all_to_all | solution.py:415
  19.4 210.0 %collective-permute-start.1 = (bf16[1,2,768,128]{3,2,1,0:T(8,128)(2,1)}, bf16[1,2,768,128]{3,2,1,0:T(8,128)(2,1)}, u32[]{:S(2)}, u32[]{:S(2)}) collective-permute-start(bf16[1,2,768,128]{3,2,1,0:T(8,128)(2,1)} %get-tuple-element.31), channel_id=1, source_target_pairs={{0,1},{1,0},{2,3},{3,2},{4,5},{5,4},{6,7},{7,6},{8,9},{9,8},{10,11... | collective-permute-start | bytes 1179656 | tf_op jit(solution)/shard_map/ppermute | solution.py:424
  19.4 124.5 %collective-permute-start.3 = (bf16[1,2,768,128]{3,2,1,0:T(8,128)(2,1)}, bf16[1,2,768,128]{3,2,1,0:T(8,128)(2,1)}, u32[]{:S(2)}, u32[]{:S(2)}) collective-permute-start(bf16[1,2,768,128]{3,2,1,0:T(8,128)(2,1)} %get-tuple-element.42), channel_id=1, source_target_pairs={{0,1},{1,0},{2,3},{3,2},{4,5},{5,4},{6,7},{7,6},{8,9},{9,8},{10,11... | collective-permute-start | bytes 1179656 | tf_op jit(solution)/shard_map/ppermute | solution.py:424
  21.4 73.4 %collective-permute-start.4 = (bf16[2,2,768,128]{3,2,1,0:T(8,128)(2,1)}, bf16[2,2,768,128]{3,2,1,0:T(8,128)(2,1)S(1)}, u32[]{:S(2)}, u32[]{:S(2)}) collective-permute-start(bf16[2,2,768,128]{3,2,1,0:T(8,128)(2,1)} %get-tuple-element.45), channel_id=1, source_target_pairs={{0,1},{1,0},{2,3},{3,2},{4,5},{5,4},{6,7},{7,6},{8,9},{9,8},{10,11... | collective-permute-start | bytes 2359304 | tf_op jit(solution)/shard_map/ppermute | solution.py:424
  21.5 95.7 %collective-permute-start.6 = (bf16[2,2,768,128]{3,2,1,0:T(8,128)(2,1)}, bf16[2,2,768,128]{3,2,1,0:T(8,128)(2,1)S(1)}, u32[]{:S(2)}, u32[]{:S(2)}) collective-permute-start(bf16[2,2,768,128]{3,2,1,0:T(8,128)(2,1)} %get-tuple-element.53), channel_id=1, source_target_pairs={{0,1},{1,0},{2,3},{3,2},{4,5},{5,4},{6,7},{7,6},{8,9},{9,8},{10,11... | collective-permute-start | bytes 2359304 | tf_op jit(solution)/shard_map/ppermute | solution.py:424
  23.5 73.7 %collective-permute-start = (bf16[8,2,256,128]{3,2,1,0:T(8,128)(2,1)S(1)}, bf16[8,2,256,128]{3,2,1,0:T(8,128)(2,1)S(1)}, u32[]{:S(2)}, u32[]{:S(2)}) collective-permute-start(bf16[8,2,256,128]{3,2,1,0:T(8,128)(2,1)S(1)} %copy-done.5), channel_id=1, source_target_pairs={{0,1},{1,0},{2,3},{3,2},{4,5},{5,4},{6,7},{7,6},{8,9},{9,8},{10,11... | collective-permute-start | bytes 3145736 | tf_op jit(solution)/shard_map/ppermute | solution.py:420
  59.1 35.8 %copy-start.6 = (bf16[2,2,768,128]{3,2,1,0:T(8,128)(2,1)S(1)}, bf16[2,2,768,128]{3,2,1,0:T(8,128)(2,1)}, u32[]{:S(2)}) copy-start(bf16[2,2,768,128]{3,2,1,0:T(8,128)(2,1)} %get-tuple-element.48) | copy-start | bytes 2359300
  94.8 2.3 copy-start.8
  94.9 145.3 %collective-permute-start.5 = (bf16[2,2,768,128]{3,2,1,0:T(8,128)(2,1)S(1)}, bf16[2,2,768,128]{3,2,1,0:T(8,128)(2,1)}, u32[]{:S(2)}, u32[]{:S(2)}) collective-permute-start(bf16[2,2,768,128]{3,2,1,0:T(8,128)(2,1)S(1)} %copy-done.6), channel_id=1, source_target_pairs={{0,1},{1,0},{2,3},{3,2},{4,5},{5,4},{6,7},{7,6},{8,9},{9,8},{10,11... | collective-permute-start | bytes 2359304 | tf_op jit(solution)/shard_map/ppermute | solution.py:424
  97.1 1.0 copy-start.4
  117.1 0.9 copy-start.7
  137.0 17.5 %copy-start = (bf16[8,3,256,128]{3,2,1,0:T(8,128)(2,1)}, bf16[8,3,256,128]{3,2,1,0:T(8,128)(2,1)S(1)}, u32[]{:S(2)}) copy-start(bf16[8,3,256,128]{3,2,1,0:T(8,128)(2,1)S(1)} %all-to-all-done.refs_0_.refs_1_.refs_2_.q_ref.ka.va) | copy-start | bytes 4718596
  137.0 47.9 %all-to-all-start.1 = ((bf16[8,2,256,128]{3,2,1,0:T(8,128)(2,1)}), bf16[8,2,256,128]{3,2,1,0:T(8,128)(2,1)S(1)}, u32[]{:S(2)}, u32[]{:S(2)}) async-start(bf16[8,2,256,128]{3,2,1,0:T(8,128)(2,1)} %copy-done.4), calls=%async_computation.1 | async-start | bytes 2097152 | tf_op jit(solution)/shard_map/all_to_all | solution.py:415
  185.0 1.9 copy-start.2
  185.0 32.6 %collective-permute-start.2 = (bf16[16,2,32,128]{3,2,1,0:T(8,128)(2,1)S(1)}, bf16[16,2,32,128]{3,2,1,0:T(8,128)(2,1)S(1)}, u32[]{:S(2)}, u32[]{:S(2)}) collective-permute-start(bf16[16,2,32,128]{3,2,1,0:T(8,128)(2,1)S(1)} %pad_maximum_fusion), channel_id=1, source_target_pairs={{0,16},{1,17},{2,18},{3,19},{4,20},{5,21},{6,22},{7,23},{8,24},{9,... | collective-permute-start | bytes 786440 | tf_op jit(solution)/shard_map/ppermute | solution.py:431
  217.6 0.7 copy-start.3
  222.4 36.7 %all-to-all-start.2 = ((bf16[8,160,256]{2,1,0:T(8,128)(2,1)}), bf16[8,160,256]{2,1,0:T(8,128)(2,1)S(1)}, u32[]{:S(2)}, u32[]{:S(2)}) async-start(bf16[8,160,256]{2,1,0:T(8,128)(2,1)} %far.1), calls=%async_computation.2 | async-start | bytes 1310720 | tf_op jit(solution)/shard_map/all_to_all | solution.py:415
  259.2 1.0 copy-start.1

commit v2 on v1

--- a/solution.py
+++ b/solution.py
@@ -16,13 +16,14 @@
 TOK = 1024
 MID = 256
 FAR = 32
-CHUNKS = ((0, 2), (2, 2), (4, 2), (6, 1), (7, 1))
-RET = 160
-VMEM = 56 * 2**20
-
-
-def params(axes):
-    return pltpu.CompilerParams(dimension_semantics=("arbitrary",) * axes, vmem_limit_bytes=VMEM)
+CHUNKS = ((0, 2), (2, 3), (5, 2), (7, 1))
+RET = 176
+WIDE = 56 * 2**20
+SLIM = 30 * 2**20
+
+
+def params(axes, limit=WIDE):
+    return pltpu.CompilerParams(dimension_semantics=("arbitrary",) * axes, vmem_limit_bytes=limit)
 
 
 def token_class(slot, head):
@@ -38,43 +39,46 @@
     return (b == 32 * (a % 8) + a // 8).astype(F32).astype(BF)
 
 
-def prep_kernel(q_ref, k_ref, v_ref, qf_ref, qkvm_ref, kvm_ref, kvr_ref, *rest):
-    sent, wide = rest[:-1], rest[-1]
-    step = pl.program_id(0)
+def prep_kernel(q_ref, k_ref, v_ref, *outs):
+    for step in range(PAIRS // 2):
+
+        @pl.when(pl.program_id(0) == step)
+        def _():
+            prep_step(step, (q_ref, k_ref, v_ref), *outs)
+
+
+def prep_step(step, refs, qf_ref, qkvm_ref, kvm_ref, *sent):
     order = order_matrix(True)
     low = lax.broadcasted_iota(jnp.int32, (8, 128), 1) < 64
-    for n, ref in enumerate((q_ref, k_ref, v_ref)):
-        for t in range(4):
-            block = ref[t * 256 : (t + 1) * 256, :]
-            wide[n, t] = jnp.dot(order, block, preferred_element_type=F32)
-    for pair in range(2):
-        g = 2 * step + pair
-        lanes = slice(pair * 128, (pair + 1) * 128)
-        for slot in range(32):
-            c0 = pl.multiple_of(token_class(slot, 2 * g) * 8, 8)
-            c1 = pl.multiple_of(token_class(slot, 2 * g + 1) * 8, 8)
-            row = slot * FAR
-            for n in range(3):
+    for n, ref in enumerate(refs):
+        blocks = [
+            jnp.dot(order, ref[t * 256 : (t + 1) * 256, :], preferred_element_type=F32)
+            for t in range(4)
+        ]
+        for pair in range(2):
+            g = 2 * step + pair
+            chunk = [c for c, (first, count) in enumerate(CHUNKS) if first <= g < first + count][0]
+            at = g - CHUNKS[chunk][0]
+            lanes = slice(pair * 128, (pair + 1) * 128)
+            for slot in range(32):
+                c0 = token_class(slot, 2 * g) * 8
+                c1 = token_class(slot, 2 * g + 1) * 8
                 x = jnp.concatenate(
                     [
-                        jnp.where(low, wide[n, t, pl.ds(c0, 8), lanes], wide[n, t, pl.ds(c1, 8), lanes])
-                        for t in range(4)
+                        jnp.where(low, y[c0 : c0 + 8, lanes], y[c1 : c1 + 8, lanes])
+                        for y in blocks
                     ],
                     axis=0,
                 ).astype(BF)
+                row = slot * FAR
                 if n == 0:
                     qf_ref[pair, row : row + FAR, :] = x
                 elif slot < 8:
                     kvm_ref[pair, n - 1, row : row + FAR, :] = x
                 else:
-                    kvr_ref[pair, n - 1, row - MID : row - MID + FAR, :] = x
+                    sent[chunk][at, n - 1, row - MID : row - MID + FAR, :] = x
                 if slot < 8:
                     qkvm_ref[pair, n, row : row + FAR, :] = x
-    for (first, count), out in zip(CHUNKS, sent):
-
-        @pl.when(step == first // 2)
-        def _():
-            out[...] = kvr_ref[first % 2 : first % 2 + count]
 
 
 def prep(q, k, v):
@@ -87,17 +91,14 @@
             pl.BlockSpec((2, TOK, 128), lambda g: (g, 0, 0)),
             pl.BlockSpec((2, 3, MID, 128), lambda g: (g, 0, 0, 0)),
             pl.BlockSpec((2, 2, MID, 128), lambda g: (g, 0, 0, 0)),
-            pl.BlockSpec((2, 2, TOK - MID, 128), lambda g: (g, 0, 0, 0)),
         ]
         + [pl.BlockSpec((n, 2, TOK - MID, 128), lambda g: (0, 0, 0, 0)) for _, n in CHUNKS],
         out_shape=[
             jax.ShapeDtypeStruct((PAIRS, TOK, 128), BF),
             jax.ShapeDtypeStruct((PAIRS, 3, MID, 128), BF),
             jax.ShapeDtypeStruct((PAIRS, 2, MID, 128), BF),
-            jax.ShapeDtypeStruct((PAIRS, 2, TOK - MID, 128), BF),
         ]
         + [jax.ShapeDtypeStruct((n, 2, TOK - MID, 128), BF) for _, n in CHUNKS],
-        scratch_shapes=[pltpu.VMEM((3, 4, 256, 256), F32)],
         compiler_params=params(1),
         name="prep",
     )(q, k, v)
@@ -137,9 +138,16 @@
 def attend_kernel(*refs, parts, carried, qb, qt):
     q_ref, refs = refs[0], refs[1:]
     k_refs, v_refs, refs = refs[:parts], refs[parts : 2 * parts], refs[2 * parts :]
+    carry = None
     if carried:
-        oi_ref, mi_ref, refs = refs[0], refs[1], refs[2:]
-    o_ref, m_ref, vt = refs
+        carry, refs = refs[:2], refs[2:]
+    attend_body(q_ref, k_refs, v_refs, carry, *refs, qb, qt)
+
+
+def attend_body(q_ref, k_refs, v_refs, carry, o_ref, m_ref, vt, qb, qt):
+    carried = carry is not None
+    if carried:
+        oi_ref, mi_ref = carry
 
     @pl.when(pl.program_id(1) == 0)
     def _():
@@ -165,7 +173,7 @@
 
     @pl.when(jnp.min(safe) < 0.5)
     def _():
-        def shifted(n, carry):
+        def shifted(n, state):
             e = n % 2
             cols = pl.ds(pl.multiple_of((n // 2) * 256, 256), 256)
             heads = pl.ds(pl.multiple_of(e * 64, 64), 64)
@@ -186,25 +194,30 @@
             o_ref[0, heads, cols] = o
             m_ref[0, 2 * e, :, cols] = peak
             m_ref[0, 2 * e + 1, :, cols] = den
-            return carry
+            return state
 
         lax.fori_loop(0, 2 * (qb // 256), shifted, 0)
 
 
-def attend(groups, nq, qb, qt, query, parts, carry=None, carry_first=0):
+def carry_specs(first, qb):
+    return [
+        pl.BlockSpec((1, 128, qb), lambda g, j: (g + first, 0, j)),
+        pl.BlockSpec((1, 4, 1, qb), lambda g, j: (g + first, 0, 0, j)),
+    ]
+
+
+def attend(groups, nq, qb, qt, query, parts, carry=None, first=None, limit=WIDE):
     nk = sum(p[3] for p in parts)
     specs = [query[1]] + [p[1] for p in parts] + [p[2] for p in parts]
-    args = [query[0]] + [p[0] for p in parts] + [p[0] for p in parts]
-
-    def carry_specs(first):
-        return [
-            pl.BlockSpec((1, 128, qb), lambda g, j: (g + first, 0, j)),
-            pl.BlockSpec((1, 4, 1, qb), lambda g, j: (g + first, 0, 0, j)),
-        ]
-
+    args = [query[0]] + [p[0] for p in parts] + [p[4] if len(p) > 4 else p[0] for p in parts]
+
+    alias = {}
+    if first is not None:
+        alias = {len(args): 0, len(args) + 1: 1}
     if carry is not None:
-        specs += carry_specs(carry_first)
+        specs += carry_specs(first or 0, qb)
         args += list(carry)
+    total = groups if first is None else carry[0].shape[0]
     exps = groups * 2 * nq * nk
     return pl.pallas_call(
         functools.partial(
@@ -212,38 +225,42 @@
         ),
         grid=(groups, nq // qb),
         in_specs=specs,
-        out_specs=carry_specs(0),
+        out_specs=carry_specs(first or 0, qb),
         out_shape=[
-            jax.ShapeDtypeStruct((groups, 128, nq), F32),
-            jax.ShapeDtypeStruct((groups, 4, 1, nq), F32),
+            jax.ShapeDtypeStruct((total, 128, nq), F32),
+            jax.ShapeDtypeStruct((total, 4, 1, nq), F32),
         ],
         scratch_shapes=[pltpu.VMEM((2, 80, nk), BF)],
-        compiler_params=params(2),
+        input_output_aliases=alias,
+        compiler_params=params(2, limit),
         cost_estimate=pl.CostEstimate(
             flops=exps * 1100, bytes_accessed=groups * (nq + nk) * 1024, transcendentals=exps
         ),
     )(*args)
 
 
-def near(first, count, qf, kvm, kvr, kvr_first, carry=None, carry_first=0):
-    def part(array, base, rows):
-        return (
-            array,
-            pl.BlockSpec((1, 1, rows, 128), lambda g, j: (g + base, 0, 0, 0)),
-            pl.BlockSpec((1, 1, rows, 128), lambda g, j: (g + base, 1, 0, 0)),
-            rows,
-        )
-
-    return attend(
-        count,
-        TOK,
-        TOK,
-        1024,
-        (qf, pl.BlockSpec((1, TOK, 128), lambda g, j: (g + first, j, 0))),
-        [part(kvm, first, MID), part(kvr, kvr_first, TOK - MID)],
-        carry,
-        carry_first,
+def near_part(array, base, rows):
+    return (
+        array,
+        pl.BlockSpec((1, 1, rows, 128), lambda g, j: (g + base, 0, 0, 0)),
+        pl.BlockSpec((1, 1, rows, 128), lambda g, j: (g + base, 1, 0, 0)),
+        rows,
     )
+
+
+def near_query(qf, first):
+    return (qf, pl.BlockSpec((1, TOK, 128), lambda g, j: (g + first, j, 0)))
+
+
+def near_here(first, count, qf, keys, values):
+    col = pl.BlockSpec((TOK, 128), lambda g, j: (0, g + first))
+    part = (keys, col, col, TOK, values)
+    return attend(count, TOK, TOK, 1024, near_query(qf, first), [part])
+
+
+def near_there(first, count, qf, kvm, kvr, carry):
+    parts = [near_part(kvm, first, MID), near_part(kvr, 0, TOK - MID)]
+    return attend(count, TOK, TOK, 1024, near_query(qf, first), parts, carry, first)
 
 
 def middle(own, keys, at, carry=None):
@@ -264,6 +281,7 @@
             )
         ],
         carry,
+        limit=SLIM,
     )
 
 
@@ -278,6 +296,7 @@
         a = mix(vt[e], jnp.exp2(s - peak).astype(BF))
         outs.append(a[:64] / a[64:65])
         levels.append(peak + jnp.log2(a[64:65]))
+    far = jnp.concatenate(outs, axis=0).T
     row = lax.broadcasted_iota(jnp.int32, (16, MID), 0)
     first = lax.broadcasted_iota(jnp.int32, (1, MID), 1) < FAR
     for d in range(PAIRS):
@@ -304,13 +323,8 @@
                 level = level - piece
                 lev = jnp.where(row == 3 * e + part, piece, lev)
         ret_ref[d, 128:144, :] = lev.astype(BF)
-        ret_ref[d, 144:160, :] = jnp.concatenate(
-            [
-                outs[b // 4][16 * (b % 4) : 16 * (b % 4) + 16, d * FAR : (d + 1) * FAR]
-                for b in range(8)
-            ],
-            axis=1,
-        ).astype(BF)
+        ret_ref[d, 144:176, 0:128] = far[d * FAR : (d + 1) * FAR].astype(BF)
+        ret_ref[d, 144:176, 128:256] = jnp.zeros((FAR, 128), BF)
 
 
 def far_and_return(own, partner, other, mid):
@@ -335,14 +349,22 @@
         out_specs=pl.BlockSpec((PAIRS, RET, MID), whole),
         out_shape=jax.ShapeDtypeStruct((PAIRS, RET, MID), BF),
         scratch_shapes=[pltpu.VMEM((2, 80, 1024), BF)],
-        compiler_params=params(1),
+        compiler_params=params(1, SLIM),
         name="far",
     )(own, own, partner, other, own, partner, other, *mid)
 
 
 def merge_kernel(o_ref, m_ref, ret_ref, *rest, first):
-    out_ref, turned = rest[-2:]
-    g = pl.program_id(0) + first
+    merge_body(o_ref, m_ref, ret_ref, *rest[-2:], pl.program_id(0) + first)
+
+
+def finish_kernel(q_ref, ka, kb, va, vb, oi_ref, mi_ref, ret_ref, *rest, first):
+    out_ref, vt, o_ref, m_ref, turned = rest[-5:]
+    attend_body(q_ref, (ka, kb), (va, vb), (oi_ref, mi_ref), o_ref, m_ref, vt, TOK, 1024)
+    merge_body(o_ref, m_ref, ret_ref, out_ref, turned, pl.program_id(0) + first)
+
+
+def merge_body(o_ref, m_ref, ret_ref, out_ref, turned, g):
     parts = []
     lev = ret_ref[0, 128:144, :].astype(F32)
     for e in range(2):
@@ -404,6 +426,34 @@
     )(*args)
 
 
+def finish(first, count, qf, kvm, kvr, carry, carry_first, ret, out):
+    query = near_query(qf, first)
+    parts = [near_part(kvm, first, MID), near_part(kvr, 0, TOK - MID)]
+    specs = [query[1]] + [p[1] for p in parts] + [p[2] for p in parts]
+    specs += carry_specs(carry_first, TOK)
+    specs += [
+        pl.BlockSpec((1, RET, MID), lambda g, j: (g + first, 0, 0)),
+        pl.BlockSpec(memory_space=pl.ANY),
+    ]
+    args = [qf, kvm, kvr, kvm, kvr, *carry, ret, out]
+    return pl.pallas_call(
+        functools.partial(finish_kernel, first=first),
+        grid=(count, 1),
+        in_specs=specs,
+        out_specs=pl.BlockSpec((TOK, 128), lambda g, j: (0, g + first)),
+        out_shape=jax.ShapeDtypeStruct((TOK, PAIRS * 128), BF),
+        scratch_shapes=[
+            pltpu.VMEM((2, 80, TOK), BF),
+            pltpu.VMEM((1, 128, TOK), F32),
+            pltpu.VMEM((1, 4, 1, TOK), F32),
+            pltpu.VMEM((TOK, 128), F32),
+        ],
+        input_output_aliases={len(args) - 1: 0},
+        compiler_params=params(2),
+        name="finish",
+    )(*args)
+
+
 GROUPS = [
     [y * 16 + x * 4 + z for x in range(4) for z in pair] for y in range(2) for pair in ((1, 2), (0, 3))
 ]
@@ -416,28 +466,27 @@
 
 
 def steps(queries, keys, values):
-    qf, qkvm, kvm, kvr, *sent = prep(queries, keys, values)
+    qf, qkvm, kvm, *sent = prep(queries, keys, values)
     kvm_there = lax.ppermute(kvm, "seq", NEAR)
     own = exchange(qkvm)
     kvr_there = []
     for part in sent:
         kvr_there.append(lax.ppermute(part, "seq", NEAR))
     partner = exchange(kvm_there)
-    half = PAIRS // 2
-    here = []
-    for i in range(2):
-        here.append(near(i * half, half, qf, kvm, kvr, i * half))
+    near = near_here(0, PAIRS, qf, keys, values)
     far_kv = jnp.concatenate([own[:, 1:, :FAR], partner[:, :, :FAR]], axis=0)
     other = lax.ppermute(far_kv, "seq", PLANE)
     mid = middle(own, own, 1)
     mid = middle(own, partner, 0, mid)
     ret = far_and_return(own, partner, other, mid)
     ret = exchange(ret)
-    far_rows = ret[:, 144:, :].reshape(PAIRS, 16, 8, FAR).transpose(3, 0, 2, 1).reshape(FAR, PAIRS * 128)
-    out = None
-    for i, (a, n) in enumerate(CHUNKS):
-        both = near(a, n, qf, kvm_there, kvr_there[i], 0, here[a // half], a % half)
-        out = merge(a, n, both, ret, out)
+    far_rows = ret[:, 144:, :128].transpose(1, 0, 2).reshape(FAR, PAIRS * 128)
+    for i in (0, 1):
+        near = near_there(*CHUNKS[i], qf, kvm_there, kvr_there[i], near)
+    out = merge(0, CHUNKS[2][0], near, ret, None)
+    for i in (2, 3):
+        a, n = CHUNKS[i]
+        out = finish(a, n, qf, kvm_there, kvr_there[i], near, a, ret, out)
     return out, far_rows
 
 

time: 274 us -> 258 us (0.942)
  Pallas kernels: 238 us -> 220 us
  local copies, waits for them, and re-layouts: 3.55 us -> 7.11 us
    pallas_call x9 -> x5, Pallas kernels: 211 us -> 173 us  [attend(): pl.pallas_call(functools.partial(attend_kernel, parts=len(parts), carried...]
    pallas_call x0 -> x2, Pallas kernels: none -> 31 us  [finish(): pl.pallas_call(functools.partial(finish_kernel, first=first), grid=(count...]
    pallas_call x5 -> x1, Pallas kernels: 13 us -> 5.75 us  [merge(): pl.pallas_call(functools.partial(merge_kernel, first=first), grid=(count,...]
    pallas_call x1, Pallas kernels: 10.3 us -> 7.52 us  [prep(): pl.pallas_call(prep_kernel, grid=(PAIRS // 2,), in_specs=[col, col, col],...]
    ppermute x5 -> x4, starting transfers between devices: 6.31 us -> 4.05 us  [steps(): kvr_there.append(lax.ppermute(part, 'seq', NEAR))]
  transfers between devices with their start and end apart: 10 -> 9, of which waited for: 0 -> 0; matrix products, arithmetic and copies ran while one was open for 0% -> 1% of each run, Pallas kernels for 79% -> 78%
where the time goes in v2:
time: 258 us; the launch traced here: 257 us
  Pallas kernels  220 us (85%)
  starting transfers between devices  28.5 us (11%)
  local copies, waits for them, and re-layouts  7.11 us (3%)
    pallas_call x5, Pallas kernels, attend(): pl.pallas_call(functools.partial(attend_kernel, parts=len(parts), carried...  173 us
    pallas_call x2, Pallas kernels, finish(): pl.pallas_call(functools.partial(finish_kernel, first=first), grid=(count...  31 us
    all_to_all x3, starting transfers between devices, exchange(): return lax.all_to_all(x, 'seq', 0, 0, axis_index_groups=GROUPS, tiled=True)  20.6 us
    pallas_call x1, Pallas kernels, prep(): pl.pallas_call(prep_kernel, grid=(PAIRS // 2,), in_specs=[col, col, col],...  7.52 us
    pallas_call x1, Pallas kernels, merge(): pl.pallas_call(functools.partial(merge_kernel, first=first), grid=(count,...  5.75 us
  transfers between devices with their start and end apart: 9, of which 0 were waited for; matrix products, arithmetic and copies ran while one was open for 1% of the time, Pallas kernels for 78%

profile of v2, /device:TPU:2, one launch (start us, length us, event | category | flops | bytes accessed | tf_op | source)
XLA Modules:
  0.0 257.0 jit_solution(7269515528492891707)
XLA Ops:
  0.6 7.5 %prep.1 = (bf16[8,1024,128]{2,1,0:T(8,128)(2,1)}, bf16[8,3,256,128]{3,2,1,0:T(8,128)(2,1)}, bf16[8,2,256,128]{3,2,1,0:T(8,128)(2,1)}, bf16[2,2,768,128]{3,2,1,0:...) custom-call(bf16[1024,1024]{1,0:T(8,128)(2,1)} %q_ref.1, ...), custom_call_target="tpu_custom_call" | custom-call | tf_op jit(solution)/shard_map/prep/pallas_call | solution.py:86
  8.2 2.0 collective-permute-start
  10.2 6.8 %all-to-all-start = ((bf16[8,3,256,128]{3,2,1,0:T(8,128)(2,1)}), bf16[8,3,256,128]{3,2,1,0:T(8,128)(2,1)S(1)}, u32[]{:S(2)}, u32[]{:S(2)}) async-start(bf16[8,3,256,128]{3,2,1,0:T(8,128)(2,1)} %get-tuple-element.30), calls=%async_computation | async-start | bytes 3145728 | tf_op jit(solution)/shard_map/all_to_all | solution.py:465
  16.9 1.0 collective-permute-start.3
  18.0 1.0 collective-permute-start.2
  19.0 1.0 collective-permute-start.5
  20.0 1.0 collective-permute-start.1
  21.0 69.1 %shard_map.50 = (f32[8,128,1024]{2,1,0:T(8,128)}, f32[8,4,1,1024]{3,2,1,0:T(1,128)}) custom-call(bf16[8,1024,128]{2,1,0:T(8,128)(2,1)} %get-tuple-element.19.refs_0_.q_ref, bf16[1024,1024]{1,0:T(8,128)(2,1)} %refs_1_.1, bf16[1024,1024]{1,0:T(8,128)(2,1)} %refs_2_.1), custom_call_target="tpu_custom_call" | custom-call | flops 18454937600 | bytes 16777216 | tf_op jit(solution)/shard_map/pallas_call | solution.py:222
  90.1 0.0 collective-permute-done.refs_1_.refs_3_.ka.va
  90.2 1.0 copy-done.2
  91.2 0.0 all-to-all-done.refs_0_.refs_1_.refs_2_.q_ref.ka.va
  91.2 6.9 %all-to-all-start.1 = ((bf16[8,2,256,128]{3,2,1,0:T(8,128)(2,1)}), bf16[8,2,256,128]{3,2,1,0:T(8,128)(2,1)S(1)}, u32[]{:S(2)}, u32[]{:S(2)}) async-start(bf16[8,2,256,128]{3,2,1,0:T(8,128)(2,1)} %copy-done.2), calls=%async_computation.1 | async-start | bytes 2097152 | tf_op jit(solution)/shard_map/all_to_all | solution.py:465
  98.1 19.0 %shard_map.51 = (f32[8,128,1024]{2,1,0:T(8,128)}, f32[8,4,1,1024]{3,2,1,0:T(1,128)}) custom-call(bf16[8,1024,128]{2,1,0:T(8,128)(2,1)} %get-tuple-element.19.refs_0_.q_ref, bf16[8,2,256,128]{3,2,1,0:T(8,128)(2,1)} %copy-done.2, bf16[2,2,768,128]{3,2,1,0:T(8,128)(2,1)} %collective-permute-done.3.refs_2_.refs_4_, ...), custom_call_target="tpu_custom_call", output_to_operand_aliasing={{0}: (5, {}), {1}: (6, {})} | custom-call | flops 4613734400 | bytes 4194304 | tf_op jit(solution)/shard_map/pallas_call | solution.py:222
  117.1 28.5 %shard_map.53 = (f32[1,128,2048]{2,1,0:T(8,128)S(1)}, f32[1,4,1,2048]{3,2,1,0:T(1,128)S(1)}) custom-call(bf16[8,3,256,128]{3,2,1,0:T(8,128)(2,1)S(1)} %all-to-all-done.refs_0_.refs_1_.refs_2_.q_ref.ka.va, bf16[8,3,256,128]{3,2,1,0:T(8,128)(2,1)S(1)} %all-to-all-done.refs_0_.refs_1_.refs_2_.q_ref.ka.va, ...), custom_call_target="tpu_custom_call" | custom-call | flops 9227468800 | bytes 4194304 | tf_op jit(solution)/shard_map/pallas_call | solution.py:222
  145.6 0.0 copy-start
  145.6 1.0 copy-done
  146.6 0.7 slice.12
  147.3 0.9 pad_maximum_fusion
  148.2 1.9 collective-permute-start.4
  150.1 1.2 copy-done.1
  151.3 28.6 %shard_map.54 = (f32[1,128,2048]{2,1,0:T(8,128)S(1)}, f32[1,4,1,2048]{3,2,1,0:T(1,128)S(1)}) custom-call(bf16[8,3,256,128]{3,2,1,0:T(8,128)(2,1)S(1)} %all-to-all-done.refs_0_.refs_1_.refs_2_.q_ref.ka.va, bf16[8,2,256,128]{3,2,1,0:T(8,128)(2,1)S(1)} %all-to-all-done.1.refs_1_.refs_2_.kb.vb, ...), custom_call_target="tpu_custom_call" | custom-call | flops 9227468800 | bytes 4194304 | tf_op jit(solution)/shard_map/pallas_call | solution.py:222
  180.0 0.0 collective-permute-done.4.kc.vc
  180.0 2.7 %far.1 = bf16[8,176,256]{2,1,0:T(8,128)(2,1)} custom-call(bf16[8,3,256,128]{3,2,1,0:T(8,128)(2,1)S(1)} %all-to-all-done.refs_0_.refs_1_.refs_2_.q_ref.ka.va, bf16[8,3,256,128]{3,2,1,0:T(8,128)(2,1)S(1)} %all-to-all-done.refs_0_.refs_1_.refs_2_.q_ref.ka.va, bf16[8,2,256,128]{3,2,1,0:T(8,128)(2,1)S(1)} %all-to-all-done.1.refs_1_.refs_2_.kb.vb, ...), custom_call_target="tpu_custom_call" | custom-call | tf_op jit(solution)/shard_map/far/pallas_call | solution.py:335
  182.7 6.9 %all-to-all-start.2 = ((bf16[8,176,256]{2,1,0:T(8,128)(2,1)}), bf16[8,176,256]{2,1,0:T(8,128)(2,1)S(1)}, u32[]{:S(2)}, u32[]{:S(2)}) async-start(bf16[8,176,256]{2,1,0:T(8,128)(2,1)} %far.1), calls=%async_computation.2 | async-start | bytes 1441792 | tf_op jit(solution)/shard_map/all_to_all | solution.py:465
  189.6 0.0 collective-permute-done.2.refs_2_.refs_4_
  189.6 27.5 %shard_map.52 = (f32[8,128,1024]{2,1,0:T(8,128)}, f32[8,4,1,1024]{3,2,1,0:T(1,128)}) custom-call(bf16[8,1024,128]{2,1,0:T(8,128)(2,1)} %get-tuple-element.19.refs_0_.q_ref, bf16[8,2,256,128]{3,2,1,0:T(8,128)(2,1)} %copy-done.2, bf16[3,2,768,128]{3,2,1,0:T(8,128)(2,1)} %collective-permute-done.2.refs_2_.refs_4_, ...), custom_call_target="tpu_custom_call", output_to_operand_aliasing={{0}: (5, {}), {1}: (6, {})} | custom-call | flops 6920601600 | bytes 6291456 | tf_op jit(solution)/shard_map/pallas_call | solution.py:222
  217.0 0.9 copy-done.3
  217.9 5.8 %merge.1.rest_0_ = bf16[1024,1024]{1,0:T(8,128)(2,1)} custom-call(f32[8,128,1024]{2,1,0:T(8,128)} %get-tuple-element.28.o_ref.oi_ref, f32[8,4,1,1024]{3,2,1,0:T(1,128)} %get-tuple-element.29.m_ref.mi_ref, bf16[8,176,256]{2,1,0:T(8,128)(2,1)} %copy-done.3), custom_call_target="tpu_custom_call" | custom-call | tf_op jit(solution)/shard_map/merge/pallas_call | solution.py:416
  223.7 0.9 copy-done.4
  224.6 20.1 %finish.2.rest_0_ = bf16[1024,1024]{1,0:T(8,128)(2,1)} custom-call(bf16[8,1024,128]{2,1,0:T(8,128)(2,1)} %get-tuple-element.19.refs_0_.q_ref, bf16[8,2,256,128]{3,2,1,0:T(8,128)(2,1)} %copy-done.2, bf16[2,2,768,128]{3,2,1,0:T(8,128)(2,1)} %copy-done.4, bf16[8,2,256,128]{3,2,1,0:T(8,128)(2,1)} %copy-done.2, ...), custom_call_target="tpu_custom_call", output_to_operand_aliasing={{}: (8, {})} | custom-call | tf_op jit(solution)/shard_map/finish/pallas_call | solution.py:439
  244.7 1.5 copy_bitcast_fusion
  246.2 10.9 %finish.3 = bf16[1024,1024]{1,0:T(8,128)(2,1)} custom-call(bf16[8,1024,128]{2,1,0:T(8,128)(2,1)} %get-tuple-element.19.refs_0_.q_ref, bf16[8,2,256,128]{3,2,1,0:T(8,128)(2,1)} %copy-done.2, bf16[1,2,768,128]{3,2,1,0:T(8,128)(2,1)} %collective-permute-done.1.kb.vb, bf16[8,2,256,128]{3,2,1,0:T(8,128)(2,1)} %copy-done.2, ...), custom_call_target="tpu_custom_call", output_to_operand_aliasing={{}: (8, {})} | custom-call | tf_op jit(solution)/shard_map/finish/pallas_call | solution.py:439
  (10 shorter events, 0.0 us)
Async XLA Ops:
  8.2 82.0 %collective-permute-start = (bf16[8,2,256,128]{3,2,1,0:T(8,128)(2,1)}, bf16[8,2,256,128]{3,2,1,0:T(8,128)(2,1)S(1)}, u32[]{:S(2)}, u32[]{:S(2)}) collective-permute-start(bf16[8,2,256,128]{3,2,1,0:T(8,128)(2,1)} %get-tuple-element.20), channel_id=1, source_target_pairs={{0,1},{1,0},{2,3},{3,2},{4,5},{5,4},{6,7},{7,6},{8,9},{9,8},{10,11... | collective-permute-start | bytes 3145736 | tf_op jit(solution)/shard_map/ppermute | solution.py:470
  10.2 81.0 %all-to-all-start = ((bf16[8,3,256,128]{3,2,1,0:T(8,128)(2,1)}), bf16[8,3,256,128]{3,2,1,0:T(8,128)(2,1)S(1)}, u32[]{:S(2)}, u32[]{:S(2)}) async-start(bf16[8,3,256,128]{3,2,1,0:T(8,128)(2,1)} %get-tuple-element.30), calls=%async_computation | async-start | bytes 3145728 | tf_op jit(solution)/shard_map/all_to_all | solution.py:465
  16.9 81.1 %collective-permute-start.3 = (bf16[2,2,768,128]{3,2,1,0:T(8,128)(2,1)}, bf16[2,2,768,128]{3,2,1,0:T(8,128)(2,1)}, u32[]{:S(2)}, u32[]{:S(2)}) collective-permute-start(bf16[2,2,768,128]{3,2,1,0:T(8,128)(2,1)} %get-tuple-element.23), channel_id=1, source_target_pairs={{0,1},{1,0},{2,3},{3,2},{4,5},{5,4},{6,7},{7,6},{8,9},{9,8},{10,11... | collective-permute-start | bytes 2359304 | tf_op jit(solution)/shard_map/ppermute | solution.py:474
  18.0 171.6 %collective-permute-start.2 = (bf16[3,2,768,128]{3,2,1,0:T(8,128)(2,1)}, bf16[3,2,768,128]{3,2,1,0:T(8,128)(2,1)}, u32[]{:S(2)}, u32[]{:S(2)}) collective-permute-start(bf16[3,2,768,128]{3,2,1,0:T(8,128)(2,1)} %get-tuple-element.22), channel_id=1, source_target_pairs={{0,1},{1,0},{2,3},{3,2},{4,5},{5,4},{6,7},{7,6},{8,9},{9,8},{10,11... | collective-permute-start | bytes 3538952 | tf_op jit(solution)/shard_map/ppermute | solution.py:474
  19.0 204.7 %collective-permute-start.5 = (bf16[2,2,768,128]{3,2,1,0:T(8,128)(2,1)}, bf16[2,2,768,128]{3,2,1,0:T(8,128)(2,1)S(1)}, u32[]{:S(2)}, u32[]{:S(2)}) collective-permute-start(bf16[2,2,768,128]{3,2,1,0:T(8,128)(2,1)} %get-tuple-element.35), channel_id=1, source_target_pairs={{0,1},{1,0},{2,3},{3,2},{4,5},{5,4},{6,7},{7,6},{8,9},{9,8},{10,11... | collective-permute-start | bytes 2359304 | tf_op jit(solution)/shard_map/ppermute | solution.py:474
  20.0 226.2 %collective-permute-start.1 = (bf16[1,2,768,128]{3,2,1,0:T(8,128)(2,1)}, bf16[1,2,768,128]{3,2,1,0:T(8,128)(2,1)}, u32[]{:S(2)}, u32[]{:S(2)}) collective-permute-start(bf16[1,2,768,128]{3,2,1,0:T(8,128)(2,1)} %get-tuple-element.21), channel_id=1, source_target_pairs={{0,1},{1,0},{2,3},{3,2},{4,5},{5,4},{6,7},{7,6},{8,9},{9,8},{10,11... | collective-permute-start | bytes 1179656 | tf_op jit(solution)/shard_map/ppermute | solution.py:474
  90.1 1.0 copy-start.2
  91.2 56.1 %all-to-all-start.1 = ((bf16[8,2,256,128]{3,2,1,0:T(8,128)(2,1)}), bf16[8,2,256,128]{3,2,1,0:T(8,128)(2,1)S(1)}, u32[]{:S(2)}, u32[]{:S(2)}) async-start(bf16[8,2,256,128]{3,2,1,0:T(8,128)(2,1)} %copy-done.2), calls=%async_computation.1 | async-start | bytes 2097152 | tf_op jit(solution)/shard_map/all_to_all | solution.py:465
  145.6 1.0 copy-start
  148.2 31.8 %collective-permute-start.4 = (bf16[16,2,32,128]{3,2,1,0:T(8,128)(2,1)S(1)}, bf16[16,2,32,128]{3,2,1,0:T(8,128)(2,1)S(1)}, u32[]{:S(2)}, u32[]{:S(2)}) collective-permute-start(bf16[16,2,32,128]{3,2,1,0:T(8,128)(2,1)S(1)} %pad_maximum_fusion), channel_id=1, source_target_pairs={{0,16},{1,17},{2,18},{3,19},{4,20},{5,21},{6,22},{7,23},{8,24},{9,... | collective-permute-start | bytes 786440 | tf_op jit(solution)/shard_map/ppermute | solution.py:478
  150.1 1.2 copy-start.1
  182.7 34.4 %all-to-all-start.2 = ((bf16[8,176,256]{2,1,0:T(8,128)(2,1)}), bf16[8,176,256]{2,1,0:T(8,128)(2,1)S(1)}, u32[]{:S(2)}, u32[]{:S(2)}) async-start(bf16[8,176,256]{2,1,0:T(8,128)(2,1)} %far.1), calls=%async_computation.2 | async-start | bytes 1441792 | tf_op jit(solution)/shard_map/all_to_all | solution.py:465
  217.0 0.9 copy-start.3
  223.7 0.9 copy-start.4
